TPU v7x, 32 devices: a whole 2x2x4 slice. The times are simulated.
32 devices in a mesh: pairs: 8 (over z, y), cols: 4 (over x, core).
Axes of the slice: x: 2, y: 2, z: 4, core: 2. Of those that a mesh axis runs over, the one named last changes fastest.
Arguments:
- amplitudes: bfloat16 [64, 256, 256], P('pairs', 'cols'), may hold values from -6 to 6
- pno_counts: int32 [64], P('pairs'), may hold values from 96 to 256
- fock_blocks: bfloat16 [64, 256, 256], P('pairs'), may hold values from -1 to 5, as said below
- exchange_blocks: bfloat16 [64, 256, 256], P('pairs', 'cols'), may hold values from -6 to 6
- intersections: bfloat16 [64, 32, 256, 256], P('pairs', None, 'cols'), may hold values from -0.375 to 0.375
- partners: int32 [64, 32], P('pairs'), may hold values from 0 to 63, as said below
- couplings: float32 [64, 32], P('pairs'), may hold values from -3 to 3
Outputs:
- residual_blocks: bfloat16 [64, 256, 256], P('pairs', 'cols')
Inputs may be any that keep to these rules, and one draw needn't show every extreme that they name: `partners`: within the coupling lists of one aligned block of 8 pairs, at most 64 entries name pairs of any one aligned block of 8 pairs, and exactly 64 do for some block. `fock_blocks`: each block is symmetric.
All inputs are finite; a program needn't handle non-finite values.
Results may differ from a plain program's by a relative error of at most 0.0022.
Values may be sent and summed in bfloat16 or wider, within the bound.
No kernel may reach another device: no remote copies, remote signals or barrier semaphores. Data moves between devices by JAX's collectives and lax.ppermute only.
A program may use at most 128 MiB of HBM per device.

v0:
```python
import jax
import jax.numpy as jnp
from jax import lax
from jax.sharding import PartitionSpec as P

CPL = 32


def shards(
    amplitudes, pno_counts, fock_blocks, exchange_blocks, intersections, partners, couplings
):
    local_pairs, share, width = amplitudes.shape
    column = lax.axis_index("cols")
    row_keep = column * share + jnp.arange(share, dtype=jnp.int32)[None, :] < pno_counts[:, None]
    col_keep = jnp.arange(width, dtype=jnp.int32)[None, :] < pno_counts[:, None]
    keep = row_keep[:, :, None] & col_keep[:, None, :]
    masked = jnp.where(keep, amplitudes, jnp.zeros_like(amplitudes))
    linear = partners.reshape(-1)
    empty = jnp.zeros((local_pairs * CPL, share, width), jnp.bfloat16)
    piece = lax.all_gather(masked, "pairs", axis=0, tiled=True)
    present = (linear >= 0) & (linear < piece.shape[0])
    picked = piece[jnp.clip(linear, 0, piece.shape[0] - 1)]
    partner_flat = jnp.where(present[:, None, None], picked, empty)
    partner_blocks = partner_flat.reshape(local_pairs, CPL, share, width)
    fock_cols = lax.dynamic_slice_in_dim(fock_blocks, column * share, share, 2)
    partial_value = jnp.einsum(
        "pab,pbc->pac", fock_cols, masked, preferred_element_type=jnp.float32
    )
    whole_intersections = lax.all_gather(intersections, "cols", axis=2, tiled=True)
    projected = jnp.einsum(
        "pqab,pqbc->pqac", partner_blocks, whole_intersections, preferred_element_type=jnp.float32
    ).astype(jnp.bfloat16)
    for slot_index in range(CPL):
        term = jnp.einsum(
            "pcd,pca->pda",
            intersections[:, slot_index],
            projected[:, slot_index],
            preferred_element_type=jnp.float32,
        )
        partial_value = partial_value + couplings[:, slot_index, None, None] * term
    summed = lax.psum_scatter(partial_value, "cols", scatter_dimension=1, tiled=True)
    fock_term = jnp.einsum("pab,pbc->pac", masked, fock_blocks, preferred_element_type=jnp.float32)
    total = exchange_blocks.astype(jnp.float32) + fock_term + summed
    return jnp.where(keep, total, jnp.zeros_like(total)).astype(jnp.bfloat16)


def solution(mesh):
    in_specs = (
        P("pairs", "cols", None),
        P("pairs"),
        P("pairs", None, None),
        P("pairs", "cols", None),
        P("pairs", None, "cols", None),
        P("pairs", None),
        P("pairs", None),
    )
    out_specs = P("pairs", "cols", None)
    return jax.shard_map(shards, mesh=mesh, in_specs=in_specs, out_specs=out_specs, check_vma=False)
```

profile of v0, /device:TPU:0, one launch (start us, length us, event | category | flops | bytes accessed | tf_op | source)
XLA Modules:
  0.0 406.6 jit_solution(1802354815083428256)
XLA Ops:
  11.7 50.1 %all-gather.3.cloned.1.call-done = bf16[64,64,256]{2,1,0:T(8,128)(2,1)} async-done(((bf16[8,64,256]{2,1,0:T(8,128)(2,1)}), bf16[64,64,256]{2,1,0:T(8,128)(2,1)}) %all-gather.3.cloned.1.call-update) | async-done | bytes 2097168 | tf_op jit(solution)/shard_map/all_gather | solution.py:20
  61.9 12.4 %gather_fusion = bf16[256,64,256]{2,1,0:T(8,128)(2,1)} fusion(bf16[64,64,256]{2,1,0:T(8,128)(2,1)} %all-gather.3.cloned.1.call-done, s32[1024]{0:T(1024)S(1)} %pad_clamp_fusion), kind=kCustom, calls=%fused_computation | custom fusion | bytes 16778240 | tf_op jit(solution)/shard_map/gather | solution.py:22
  74.2 189.3 %all-gather.5.cloned.1.call-done = bf16[8,32,256,256]{3,2,1,0:T(8,128)(2,1)} async-done(((bf16[8,32,64,256]{3,2,1,0:T(8,128)(2,1)}), bf16[8,32,256,256]{3,2,1,0:T(8,128)(2,1)}) %all-gather.5.cloned.1.call-update) | async-done | bytes 33554448 | tf_op jit(solution)/shard_map/all_gather | solution.py:29
  263.5 15.6 %fusion.3 = bf16[8,32,64,256]{3,2,1,0:T(8,128)(2,1)S(1)} fusion(bf16[8,32,256,256]{3,2,1,0:T(8,128)(2,1)} %all-gather.5.cloned.1.call-done, bf16[8,32,64,256]{3,2,1,0:T(8,128)(2,1)} %bitcast.390, pred[8,32]{1,0:T(8,128)(4,1)S(1)} %compare_and_fusion), kind=kOutput, calls=%fused_computation.4 | convolution fusion | flops 2155872256 | bytes 50331904 | tf_op jit(solution)/shard_map/pqab,pqbc->pqac/dot_general | solution.py:30
  279.1 2.9 fusion.11
  282.0 2.8 fusion.12
  284.8 2.7 fusion.13
  287.6 2.9 fusion.14
  290.5 2.8 fusion.15
  293.3 2.8 fusion.16
  297.9 1.9 fusion.18
  301.6 1.8 fusion.20
  307.0 1.8 fusion.23
  308.8 1.9 fusion.24
  312.5 1.8 fusion.26
  317.9 1.9 fusion.29
  323.4 1.8 fusion.32
  327.0 1.8 fusion.34
  332.4 1.9 fusion.37
  337.9 1.8 fusion.40
  341.5 1.8 fusion.42
  343.3 23.3 %bitcast_add_fusion = f32[8,256,256]{2,1,0:T(8,128)} fusion(f32[8,256,256]{1,2,0:T(8,128)} %fusion.11, f32[8,256,256]{1,2,0:T(8,128)} %fusion.12, f32[8,256,256]{1,2,0:T(8,128)} %fusion.13, f32[8,256,256]{1,2,0:T(8,128)} %fusion.14, f32[8,256,256]{1,2,0:T(8,128)} %fusion.15, f32[8,256,256]{1,2,0:T(8,128)} %fusion.16, f32[8,256,256]{1,2,0:T(8,128)} %fusion.17, ...), kind=kOutput, calls=%fused_computation.6 | convolution fusion | flops 100663296 | bytes 70008832 | tf_op jit(solution)/shard_map/pab,pbc->pac/dot_general | solution.py:26
  366.7 31.3 %reduce-scatter.2.cloned.1.call-done = f32[8,64,256]{2,1,0:T(8,128)} async-done(((f32[8,256,256]{2,1,0:T(8,128)}), f32[8,64,256]{2,1,0:T(8,128)}) %reduce-scatter.2.cloned.1.call-update) | async-done | bytes 524304 | tf_op jit(solution)/shard_map/reduce_scatter | solution.py:41
  398.0 2.1 fusion.9
  (47 shorter events, 32.1 us)
Async XLA Ops:
  6.5 336.8 %copy-start = (bf16[8,256,256]{2,1,0:T(8,128)(2,1)S(1)}, bf16[8,256,256]{2,1,0:T(8,128)(2,1)}, u32[]{:S(2)}) copy-start(bf16[8,256,256]{2,1,0:T(8,128)(2,1)} %param.9) | copy-start | bytes 3145732
  6.5 55.3 %all-gather.3.cloned.1.call-start = ((), (), s32[]{:S(2)}) async-start(), calls=%async_computation.1 | async-start | bytes 2359296 | tf_op jit(solution)/shard_map/all_gather | solution.py:20
  9.9 0.8 copy-start.4
  9.9 0.9 copy-start.2
  9.9 253.6 %all-gather.5.cloned.1.call-start = ((), (), s32[]{:S(2)}) async-start(), calls=%async_computation.2 | async-start | bytes 41943040 | tf_op jit(solution)/shard_map/all_gather | solution.py:29
  10.7 387.3 %reduce-scatter.2.cloned.1.call-start = ((), (), s32[]{:S(2)}) async-start(), calls=%async_computation.3 | async-start | bytes 2621440 | tf_op jit(solution)/shard_map/reduce_scatter | solution.py:41
  279.1 17.0 %slice-start = ((s8[8388608]{0:T(1024)(128)(4,1)}), s8[4194304]{0:T(1024)(128)(4,1)S(1)}, s32[]{:S(2)}) async-start(s8[8388608]{0:T(1024)(128)(4,1)} %bitcast.388), calls=%async_computation.4 | async-start | bytes 8388608
  287.6 8.5 %slice-start.1 = ((s8[8388608]{0:T(1024)(128)(4,1)}), s8[4194304]{0:T(1024)(128)(4,1)S(1)}, s32[]{:S(2)}) async-start(s8[8388608]{0:T(1024)(128)(4,1)} %bitcast.388), calls=%async_computation.5 | async-start | bytes 8388608
  339.7 3.6 copy-start.1
  366.6 31.3 %copy-start.3 = (bf16[8,64,256]{2,1,0:T(8,128)(2,1)S(1)}, bf16[8,64,256]{2,1,0:T(8,128)(2,1)}, u32[]{:S(2)}) copy-start(bf16[8,64,256]{2,1,0:T(8,128)(2,1)} %param.10) | copy-start | bytes 786436
Sparse Core Ops, SparseCore 0:
  10.0 51.7 all-gather.2
  63.4 200.0 all-gather.4
  366.8 31.1 reduce-scatter.1
where the time goes:
time: 407 us
  waiting for transfers between devices  271 us (67%)
  matrix products  105 us (26%)
  local copies, waits for them, and re-layouts  13.3 us (3%)
  between operations  13.2 us (3%)
    all_gather x1, waiting for transfers between devices, shards(): lax.all_gather(intersections, 'cols', axis=2, tiled=True)  189 us
    dot_general x32, matrix products, shards(): jnp.einsum('pcd,pca->pda', intersections[:, slot_index], projected[:, slo...  64.2 us
    all_gather x1, waiting for transfers between devices, shards(): piece = lax.all_gather(masked, 'pairs', axis=0, tiled=True)  50.1 us
    reduce_scatter x1, waiting for transfers between devices, shards(): lax.psum_scatter(partial_value, 'cols', scatter_dimension=1, tiled=True)  31.3 us
    dot_general x1, matrix products, shards(): jnp.einsum('pab,pbc->pac', fock_cols, masked, preferred_element_type=jnp....  23.3 us
    dot_general x1, matrix products, shards(): jnp.einsum('pqab,pqbc->pqac', partner_blocks, whole_intersections, prefer...  15.6 us
    gather x1, local copies, waits for them, and re-layouts, shards(): picked = piece[jnp.clip(linear, 0, piece.shape[0] - 1)]  12.4 us
  transfers between devices with their start and end apart: 3, of which 3 were waited for; matrix products, arithmetic and copies ran while one was open for 3% of the time, Pallas kernels for 0%

commit v1 on v0

v1 whole, which is shorter than its diff:
```python
import functools
import jax
import jax.numpy as jnp
from jax import lax
from jax.experimental import pallas as pl
from jax.experimental.pallas import tpu as pltpu
from jax.sharding import PartitionSpec as P

GROUP = 4
CHUNKS = 4
RING_MAX = 8


def coupled_kernel(
    first, last, group, ways, own_pairs,
    slot_ref, weight_ref, info_ref, *refs,
):
    refs = list(refs)
    near = [refs.pop(0) for _ in range(group)]
    far = [refs.pop(0) for _ in range(group)]
    pieces = [refs.pop(0) for _ in range(ways)]
    if first:
        exch = [refs.pop(0) for _ in range(ways)]
        fock_ref, own_near, own_far = refs.pop(0), refs.pop(0), refs.pop(0)
    else:
        acc_ref = refs.pop(0)
    out_ref = refs.pop(0)
    whole, proj, total = refs
    share = pieces[0].shape[2]
    half = ways // 2
    pair, step = pl.program_id(0), pl.program_id(1)

    width = total.shape[0]

    def block(k):
        return info_ref[1 + 2 * own_pairs + k]

    def joined(ref):
        return ref[...].reshape(width, width)

    order = list(range(0, ways, 2)) + list(range(1, ways, 2))

    def contribution(left_near, left_far, right):
        for side, ks in ((left_near, order[:half]), (left_far, order[half:])):
            prod = jnp.dot(side, right, preferred_element_type=jnp.float32).astype(jnp.bfloat16)
            for n, k in enumerate(ks):
                proj[block(k)] = prod[n * share:(n + 1) * share]

    @pl.when(step == 0)
    def _():
        if first:
            for k in range(ways):
                proj[block(k)] = exch[k][0, 0]
            base = joined(proj).astype(jnp.float32)
            for side, ks in ((own_near, order[:half]), (own_far, order[half:])):
                for n, k in enumerate(ks):
                    whole[block(k)] = side[0, n * share:(n + 1) * share]
            own = joined(whole)
            fock = fock_ref[0]
            base = base + jnp.dot(fock, own, preferred_element_type=jnp.float32)
            total[...] = base + jnp.dot(own, fock, preferred_element_type=jnp.float32)
        else:
            total[...] = acc_ref[0]

    for g in range(group):
        for k in range(ways):
            whole[block(k)] = pieces[k][0, g]
        right = joined(whole)
        contribution(near[g][0], far[g][0], right)
        term = lax.dot_general(
            right, joined(proj), (((0,), (0,)), ((), ())), preferred_element_type=jnp.float32
        )
        weight = weight_ref[pair * (pl.num_programs(1) * group) + step * group + g]
        total[...] += weight * term

    @pl.when(step == pl.num_programs(1) - 1)
    def _():
        if last:
            count = info_ref[1 + pair]
            row = lax.broadcasted_iota(jnp.int32, (width, width), 0)
            col = lax.broadcasted_iota(jnp.int32, (width, width), 1)
            keep = (row < count) & (col < count)
            out_ref[0] = jnp.where(keep, total[...], 0.0).astype(jnp.bfloat16)
        else:
            out_ref[0] = total[...]


def run_chunk(
    start, size, first, last, near, far, own_pieces, got, slots, weights, info, acc, exch, fock
):
    own_pairs = got[0][0].shape[0]
    ways = len(got) + 1
    half_rows, width = near.shape[1], near.shape[2]
    share = own_pieces.shape[2]
    group = GROUP
    steps = size // group
    slot = lax.slice_in_dim(slots, start, start + size, axis=1).reshape(-1)
    weight = lax.slice_in_dim(weights, start, start + size, axis=1).reshape(-1)

    def partner_spec(g):
        return pl.BlockSpec(
            (1, half_rows, width),
            lambda m, s, sl, we, inf: (sl[m * (steps * group) + s * group + g], 0, 0),
        )

    in_specs = [partner_spec(g) for g in range(group)] * 2
    operands = [near] * group + [far] * group
    in_specs.append(pl.BlockSpec(
        (1, group, share, width),
        lambda m, s, sl, we, inf: (inf[0] * own_pairs + m, start // group + s, 0, 0),
    ))
    operands.append(own_pieces)
    for piece, offset in got:
        in_specs.append(pl.BlockSpec(
            (1, group, share, width),
            functools.partial(lambda o, m, s, sl, we, inf: (m, o + s, 0, 0), offset // group)))
        operands.append(piece)
    if first:
        in_specs.append(pl.BlockSpec(
            (1, 1, share, width), lambda m, s, sl, we, inf: (inf[0] * own_pairs + m, 0, 0, 0)))
        operands.append(exch[:, None])
        for piece, _ in got:
            in_specs.append(pl.BlockSpec(
                (1, 1, share, width),
                functools.partial(lambda o, m, s, sl, we, inf: (m, o, 0, 0), piece.shape[1] - 1)))
            operands.append(piece)
        in_specs.append(pl.BlockSpec(
            (1, width, width), lambda m, s, sl, we, inf: (inf[0] * own_pairs + m, 0, 0)))
        operands.append(fock)
        for array in (near, far):
            in_specs.append(pl.BlockSpec(
                (1, half_rows, width), lambda m, s, sl, we, inf: (inf[1 + own_pairs + m], 0, 0)))
            operands.append(array)
    else:
        in_specs.append(pl.BlockSpec((1, width, width), lambda m, s, sl, we, inf: (m, 0, 0)))
        operands.append(acc)
    out_type = jnp.bfloat16 if last else jnp.float32
    units = own_pairs * size
    return pl.pallas_call(
        functools.partial(coupled_kernel, first, last, group, ways, own_pairs),
        out_shape=jax.ShapeDtypeStruct((own_pairs, width, width), out_type),
        grid_spec=pltpu.PrefetchScalarGridSpec(
            num_scalar_prefetch=3,
            grid=(own_pairs, steps),
            in_specs=in_specs,
            out_specs=pl.BlockSpec((1, width, width), lambda m, s, sl, we, inf: (m, 0, 0)),
            scratch_shapes=[
                pltpu.VMEM((ways, share, width), jnp.bfloat16),
                pltpu.VMEM((ways, share, width), jnp.bfloat16),
                pltpu.VMEM((width, width), jnp.float32),
            ],
        ),
        cost_estimate=pl.CostEstimate(
            flops=units * 4 * width**3, bytes_accessed=units * 4 * width**2, transcendentals=0),
        compiler_params=pltpu.CompilerParams(dimension_semantics=("arbitrary", "arbitrary")),
        name="coupled",
    )(slot, weight, info, *operands)


def gather_pairs(half, count):
    me = lax.axis_index("pairs")
    if count > RING_MAX or count % 2:
        return lax.all_gather(half, "pairs", axis=0, tiled=True), lambda block: block
    order = list(range(0, count, 2)) + list(range(count - 1, 0, -2))
    ahead = [(order[i], order[(i + 1) % count]) for i in range(count)]
    behind = [(b, a) for a, b in ahead]
    mid = half.shape[0] // 2
    forward = backward = half
    from_ahead, from_behind = [], []
    for _ in range(1, count // 2):
        forward = lax.ppermute(forward, "pairs", ahead)
        backward = lax.ppermute(backward, "pairs", behind)
        from_behind.append(forward)
        from_ahead.append(backward)
    low = lax.ppermute(forward[:mid], "pairs", ahead)
    high = lax.ppermute(backward[mid:], "pairs", behind)
    whole = jnp.concatenate([half] + from_ahead + [low, high] + from_behind[::-1], axis=0)

    def place_of(block):
        return jnp.where(block % 2 == 0, block // 2, count - 1 - block // 2)

    return whole, lambda block: (place_of(block) - place_of(me) + count) % count


def shards(
    columns, amplitudes, pno_counts, fock_blocks, exchange_blocks, intersections, partners, couplings
):
    local_pairs, share, width = amplitudes.shape
    ways, count = columns, lax.axis_size("pairs")
    slots_per_pair = partners.shape[1]
    own_pairs = local_pairs // ways
    column = lax.axis_index("cols")
    row_keep = column * share + jnp.arange(share, dtype=jnp.int32)[None, :] < pno_counts[:, None]
    col_keep = jnp.arange(width, dtype=jnp.int32)[None, :] < pno_counts[:, None]
    keep = row_keep[:, :, None] & col_keep[:, None, :]
    masked = jnp.where(keep, amplitudes, jnp.zeros_like(amplitudes))

    def swap(array, k):
        return lax.ppermute(array, "cols", [(c, c ^ k) for c in range(ways)])

    half = jnp.concatenate(
        [masked] + [swap(masked, k) for k in range(2, ways, 2)], axis=1)

    size = slots_per_pair // CHUNKS

    def moved(k, start, stop):
        begin = (column ^ k) * own_pairs
        piece = lax.dynamic_slice(
            intersections, (begin, start, 0, 0), (own_pairs, stop - start, share, width))
        if start == 0:
            extra = lax.dynamic_slice_in_dim(exchange_blocks, begin, own_pairs, 0)
            piece = jnp.concatenate([piece, extra[:, None]], axis=1)
        return swap(piece, k)

    beside = moved(1, 0, slots_per_pair)
    got = []
    for chunk in range(CHUNKS):
        start = chunk * size
        got.append([(beside, start)] + [
            (moved(k, start, start + size), 0) for k in range(2, ways)])

    near, place = gather_pairs(half, count)
    far = swap(near, 1)

    begin = column * own_pairs
    own_partners = lax.dynamic_slice_in_dim(partners, begin, own_pairs, 0)
    weights = lax.dynamic_slice_in_dim(couplings, begin, own_pairs, 0)
    slots = place(own_partners // local_pairs) * local_pairs + own_partners % local_pairs
    own_counts = lax.dynamic_slice_in_dim(pno_counts, begin, own_pairs, 0)
    own_slots = place(lax.axis_index("pairs")) * local_pairs + begin + jnp.arange(own_pairs, dtype=jnp.int32)
    blocks = column ^ jnp.arange(ways, dtype=jnp.int32)
    info = jnp.concatenate([column[None].astype(jnp.int32), own_counts, own_slots, blocks])

    acc = None
    for chunk in range(CHUNKS):
        acc = run_chunk(
            chunk * size, size, chunk == 0, chunk == CHUNKS - 1, near, far, intersections,
            got[chunk], slots, weights, info, acc, exchange_blocks, fock_blocks)
    return lax.all_to_all(acc, "cols", split_axis=1, concat_axis=0, tiled=True)


def solution(mesh):
    in_specs = (
        P("pairs", "cols", None),
        P("pairs"),
        P("pairs", None, None),
        P("pairs", "cols", None),
        P("pairs", None, "cols", None),
        P("pairs", None),
        P("pairs", None),
    )
    out_specs = P("pairs", "cols", None)
    ways = mesh.shape["cols"]
    body = functools.partial(shards, ways)
    return jax.shard_map(body, mesh=mesh, in_specs=in_specs, out_specs=out_specs, check_vma=False)
```

time: 407 us -> 183 us (0.45)
  waiting for transfers between devices: 271 us -> 99.7 us
  matrix products: 105 us -> 0 us
  Pallas kernels: 0 us -> 27.1 us
  starting transfers between devices: 0.08 us -> 18.6 us
  between operations: 13.2 us -> 0.08 us
  blocking collectives: 0 us -> 8.97 us
  local copies, waits for them, and re-layouts: 13.3 us -> 19.7 us
  other arithmetic: 3.37 us -> 8.13 us
    all_gather x2 -> x0, waiting for transfers between devices: 239 us -> none  [the longest x1 189 us: shards(): lax.all_gather(intersections, 'cols', axis=2, tiled=True)]
    dot_general x35 -> x0, matrix products: 105 us -> none  [the longest x32 64.2 us: shards(): jnp.einsum('pcd,pca->pda', intersections[:, slot_index], projected[:, slo...]
    ppermute x0 -> x19, waiting for transfers between devices: none -> 99.7 us  [the longest x11 65.1 us: swap(): return lax.ppermute(array, 'cols', [(c, c ^ k) for c in range(ways)])]
    reduce_scatter x1 -> x0, waiting for transfers between devices: 31.3 us -> none  [shards(): lax.psum_scatter(partial_value, 'cols', scatter_dimension=1, tiled=True)]
    pallas_call x0 -> x4, Pallas kernels: none -> 27.1 us  [run_chunk(): pl.pallas_call(functools.partial(coupled_kernel, first, last, group, ways...]
    ppermute x0 -> x19, starting transfers between devices: none -> 18.6 us  [the longest x11 10.4 us: swap(): return lax.ppermute(array, 'cols', [(c, c ^ k) for c in range(ways)])]
    gather x1 -> x0, local copies, waits for them, and re-layouts: 12.4 us -> none  [shards(): picked = piece[jnp.clip(linear, 0, piece.shape[0] - 1)]]
    all_to_all x0 -> x1, blocking collectives: none -> 8.97 us  [shards(): return lax.all_to_all(acc, 'cols', split_axis=1, concat_axis=0, tiled=True)]
  transfers between devices with their start and end apart: 3 -> 19, of which waited for: 3 -> 14; matrix products, arithmetic and copies ran while one was open for 3% -> 10% of each run, Pallas kernels for 0% -> 11%
where the time goes in v1:
time: 183 us; the launch traced here: 182 us
  waiting for transfers between devices  99.7 us (54%)
  Pallas kernels  27.1 us (15%)
  local copies, waits for them, and re-layouts  19.7 us (11%)
  starting transfers between devices  18.6 us (10%)
  blocking collectives  8.97 us (5%)
  other arithmetic  8.13 us (4%)
    ppermute x11, waiting for transfers between devices, swap(): return lax.ppermute(array, 'cols', [(c, c ^ k) for c in range(ways)])  65.1 us
    ppermute x3, waiting for transfers between devices, gather_pairs(): forward = lax.ppermute(forward, 'pairs', ahead)  31.2 us
    pallas_call x4, Pallas kernels, run_chunk(): pl.pallas_call(functools.partial(coupled_kernel, first, last, group, ways...  27.1 us
    ppermute x11, starting transfers between devices, swap(): return lax.ppermute(array, 'cols', [(c, c ^ k) for c in range(ways)])  10.4 us
    all_to_all x1, blocking collectives, shards(): return lax.all_to_all(acc, 'cols', split_axis=1, concat_axis=0, tiled=True)  8.97 us
    unnamed x19, local copies, waits for them, and re-layouts  5.82 us
    dynamic_slice x2, local copies, waits for them, and re-layouts, moved(): lax.dynamic_slice(intersections, (begin, start, 0, 0), (own_pairs, stop -...  5.78 us
    ppermute x3, starting transfers between devices, gather_pairs(): forward = lax.ppermute(forward, 'pairs', ahead)  4.77 us
  transfers between devices with their start and end apart: 19, of which 14 were waited for; matrix products, arithmetic and copies ran while one was open for 10% of the time, Pallas kernels for 11%

profile of v1, /device:TPU:0, one launch (start us, length us, event | category | flops | bytes accessed | tf_op | source)
XLA Modules:
  0.0 182.3 jit_solution(14486613706024130120)
XLA Ops:
  2.6 3.0 %collective-permute-start = (bf16[8,64,256]{2,1,0:T(8,128)(2,1)S(1)}, bf16[8,64,256]{2,1,0:T(8,128)(2,1)S(1)}, u32[]{:S(2)}, u32[]{:S(2)}) collective-permute-start(bf16[8,64,256]{2,1,0:T(8,128)(2,1)S(1)} %and_select_fusion), channel_id=1, source_target_pairs={{0,2},{1,3},{2,0},{3,1},{4,6},{5,7},{6,4},{7,5},{8,10},{9,11},{10,... | collective-permute-start | bytes 786440 | tf_op jit(solution)/shard_map/ppermute | solution.py:199
  5.6 6.3 %collective-permute-done = bf16[8,64,256]{2,1,0:T(8,128)(2,1)S(1)} collective-permute-done((bf16[8,64,256]{2,1,0:T(8,128)(2,1)S(1)}, bf16[8,64,256]{2,1,0:T(8,128)(2,1)S(1)}, u32[]{:S(2)}, u32[]{:S(2)}) %collective-permute-start) | collective-permute-done | bytes 262176 | tf_op jit(solution)/shard_map/ppermute | solution.py:199
  12.8 1.8 %collective-permute-start.4 = (bf16[8,128,256]{2,1,0:T(8,128)(2,1)S(1)}, bf16[8,128,256]{2,1,0:T(8,128)(2,1)S(1)}, u32[]{:S(2)}, u32[]{:S(2)}) collective-permute-start(bf16[8,128,256]{2,1,0:T(8,128)(2,1)S(1)} %get-tuple-element.13), channel_id=1, source_target_pairs={{0,8},{8,16},{16,24},{24,28},{28,20},{20,12},{12,4},{4,0},{1,9},{9... | collective-permute-start | bytes 1572872 | tf_op jit(solution)/shard_map/ppermute | solution.py:171
  14.9 11.1 %collective-permute-done.4 = bf16[8,128,256]{2,1,0:T(8,128)(2,1)S(1)} collective-permute-done((bf16[8,128,256]{2,1,0:T(8,128)(2,1)S(1)}, bf16[8,128,256]{2,1,0:T(8,128)(2,1)S(1)}, u32[]{:S(2)}, u32[]{:S(2)}) %collective-permute-start.4) | collective-permute-done | bytes 524320 | tf_op jit(solution)/shard_map/ppermute | solution.py:171
  28.0 10.2 %collective-permute-done.5 = bf16[8,128,256]{2,1,0:T(8,128)(2,1)S(1)} collective-permute-done((bf16[8,128,256]{2,1,0:T(8,128)(2,1)S(1)}, bf16[8,128,256]{2,1,0:T(8,128)(2,1)S(1)}, u32[]{:S(2)}, u32[]{:S(2)}) %collective-permute-start.5) | collective-permute-done | bytes 524320 | tf_op jit(solution)/shard_map/ppermute | solution.py:171
  40.2 10.0 %collective-permute-done.6 = bf16[8,128,256]{2,1,0:T(8,128)(2,1)S(1)} collective-permute-done((bf16[8,128,256]{2,1,0:T(8,128)(2,1)S(1)}, bf16[8,128,256]{2,1,0:T(8,128)(2,1)S(1)}, u32[]{:S(2)}, u32[]{:S(2)}) %collective-permute-start.6) | collective-permute-done | bytes 524320 | tf_op jit(solution)/shard_map/ppermute | solution.py:171
  54.9 1.7 collective-permute-done.7
  57.3 1.6 collective-permute-done.8
  62.2 1.7 constant_dynamic-slice_fusion.8
  64.0 1.6 pad_maximum_fusion
  66.1 4.0 %constant_dynamic-slice_fusion = (bf16[2,8,64,256]{3,2,1,0:T(8,128)(2,1)S(1)}, bf16[2,8,64,256]{3,2,1,0:T(8,128)(2,1)S(1)}, bf16[2,8,64,256]{3,2,1,0:T(8,128)(2,...) fusion(bf16[8,32,64,256]{3,2,1,0:T(8,128)(2,1)} %refs_8_.7, ...), kind=kLoop, calls=%fused_computation.18 | loop fusion | bytes 8388616 | tf_op jit(solution)/shard_map/dynamic_slice | solution.py:208
  75.2 10.0 %collective-permute-done.15.refs_10_ = bf16[2,8,64,256]{3,2,1,0:T(8,128)(2,1)} collective-permute-done((bf16[2,8,64,256]{3,2,1,0:T(8,128)(2,1)}, bf16[2,8,64,256]{3,2,1,0:T(8,128)(2,1)}, u32[]{:S(2)}, u32[]{:S(2)}) %collective-permute-start.15) | collective-permute-done | bytes 524320 | tf_op jit(solution)/shard_map/ppermute | solution.py:199
  90.4 7.4 %collective-permute-done.17.refs_10_.refs_14_ = bf16[2,9,64,256]{3,2,1,0:T(8,128)(2,1)S(1)} collective-permute-done((bf16[2,9,64,256]{3,2,1,0:T(8,128)(2,1)}, bf16[2,9,64,256]{3,2,1,0:T(8,128)(2,1)S(1)}, u32[]{:S(2)}, u32[]{:S(2)}) %collective-permute-start.17) | collective-permute-done | bytes 589856 | tf_op jit(solution)/shard_map/ppermute | solution.py:199
  99.3 10.3 %collective-permute-done.18.refs_11_.refs_15_ = bf16[2,9,64,256]{3,2,1,0:T(8,128)(2,1)S(1)} collective-permute-done((bf16[2,9,64,256]{3,2,1,0:T(8,128)(2,1)}, bf16[2,9,64,256]{3,2,1,0:T(8,128)(2,1)S(1)}, u32[]{:S(2)}, u32[]{:S(2)}) %collective-permute-start.18) | collective-permute-done | bytes 589856 | tf_op jit(solution)/shard_map/ppermute | solution.py:199
  109.5 2.2 %collective-permute-start.14 = (bf16[2,8,64,256]{3,2,1,0:T(8,128)(2,1)}, bf16[2,8,64,256]{3,2,1,0:T(8,128)(2,1)}, u32[]{:S(2)}, u32[]{:S(2)}) collective-permute-start(bf16[2,8,64,256]{3,2,1,0:T(8,128)(2,1)} %get-tuple-element.9), channel_id=1, source_target_pairs={{0,3},{1,2},{2,1},{3,0},{4,7},{5,6},{6,5},{7,4},{8,11},{9,10},{10,... | collective-permute-start | bytes 1572872 | tf_op jit(solution)/shard_map/ppermute | solution.py:199
  113.1 7.2 %coupled.4.refs_12_ = f32[2,256,256]{2,1,0:T(8,128)} custom-call(s32[16]{0:T(128)} %reshape.78.slot_ref, f32[16]{0:T(128)} %reshape.79.weight_ref, s32[9]{0:T(128)} %pad_add_fusion.info_ref, bf16[64,128,256]{2,1,0:T(8,128)(2,1)} %constant_dynamic-update-slice_fusion.refs_0_.refs_1_.refs_2_.refs_3_.refs_17_, ...), custom_call_target="tpu_custom_call" | custom-call | flops 1073741824 | bytes 4194304 | tf_op jit(solution)/shard_map/coupled/pallas_call | solution.py:139
  120.8 6.6 %coupled.5.refs_12_ = f32[2,256,256]{2,1,0:T(8,128)} custom-call(s32[16]{0:T(128)} %reshape.76.slot_ref, f32[16]{0:T(128)} %reshape.77.weight_ref, s32[9]{0:T(128)} %pad_add_fusion.info_ref, bf16[64,128,256]{2,1,0:T(8,128)(2,1)} %constant_dynamic-update-slice_fusion.refs_0_.refs_1_.refs_2_.refs_3_.refs_17_, ...), custom_call_target="tpu_custom_call" | custom-call | flops 1073741824 | bytes 4194304 | tf_op jit(solution)/shard_map/coupled/pallas_call | solution.py:139
  127.4 5.6 %collective-permute-done.13.refs_10_ = bf16[2,8,64,256]{3,2,1,0:T(8,128)(2,1)} collective-permute-done((bf16[2,8,64,256]{3,2,1,0:T(8,128)(2,1)}, bf16[2,8,64,256]{3,2,1,0:T(8,128)(2,1)}, u32[]{:S(2)}, u32[]{:S(2)}) %collective-permute-start.13) | collective-permute-done | bytes 524320 | tf_op jit(solution)/shard_map/ppermute | solution.py:199
  133.0 10.2 %collective-permute-done.14.refs_11_ = bf16[2,8,64,256]{3,2,1,0:T(8,128)(2,1)} collective-permute-done((bf16[2,8,64,256]{3,2,1,0:T(8,128)(2,1)}, bf16[2,8,64,256]{3,2,1,0:T(8,128)(2,1)}, u32[]{:S(2)}, u32[]{:S(2)}) %collective-permute-start.14) | collective-permute-done | bytes 524320 | tf_op jit(solution)/shard_map/ppermute | solution.py:199
  143.2 6.6 %coupled.6.refs_12_ = f32[2,256,256]{2,1,0:T(8,128)} custom-call(s32[16]{0:T(128)} %reshape.74.slot_ref, f32[16]{0:T(128)} %reshape.75.weight_ref, s32[9]{0:T(128)} %pad_add_fusion.info_ref, bf16[64,128,256]{2,1,0:T(8,128)(2,1)} %constant_dynamic-update-slice_fusion.refs_0_.refs_1_.refs_2_.refs_3_.refs_17_, ...), custom_call_target="tpu_custom_call" | custom-call | flops 1073741824 | bytes 4194304 | tf_op jit(solution)/shard_map/coupled/pallas_call | solution.py:139
  149.9 5.6 %collective-permute-done.11.refs_10_ = bf16[2,8,64,256]{3,2,1,0:T(8,128)(2,1)} collective-permute-done((bf16[2,8,64,256]{3,2,1,0:T(8,128)(2,1)}, bf16[2,8,64,256]{3,2,1,0:T(8,128)(2,1)}, u32[]{:S(2)}, u32[]{:S(2)}) %collective-permute-start.11) | collective-permute-done | bytes 524320 | tf_op jit(solution)/shard_map/ppermute | solution.py:199
  155.5 9.3 %collective-permute-done.12.refs_11_ = bf16[2,8,64,256]{3,2,1,0:T(8,128)(2,1)} collective-permute-done((bf16[2,8,64,256]{3,2,1,0:T(8,128)(2,1)}, bf16[2,8,64,256]{3,2,1,0:T(8,128)(2,1)}, u32[]{:S(2)}, u32[]{:S(2)}) %collective-permute-start.12) | collective-permute-done | bytes 524320 | tf_op jit(solution)/shard_map/ppermute | solution.py:199
  164.8 6.6 %coupled.7 = bf16[2,256,256]{2,1,0:T(8,128)(2,1)} custom-call(s32[16]{0:T(128)} %reshape.72.slot_ref, f32[16]{0:T(128)} %reshape.73.weight_ref, s32[9]{0:T(128)} %pad_add_fusion.info_ref, bf16[64,128,256]{2,1,0:T(8,128)(2,1)} %constant_dynamic-update-slice_fusion.refs_0_.refs_1_.refs_2_.refs_3_.refs_17_, ...), custom_call_target="tpu_custom_call" | custom-call | flops 1073741824 | bytes 4194304 | tf_op jit(solution)/shard_map/coupled/pallas_call | solution.py:139
  172.6 9.0 %all_to_all.18 = bf16[2,256,256]{2,0,1:T(2,128)(2,1)S(1)} all-to-all(bf16[2,256,256]{2,0,1:T(2,128)(2,1)S(1)} %copy.9), channel_id=1, replica_groups=mesh['pairs'=8,'cols'=4] {'cols'}, dimensions={1} | all-to-all | bytes 524288 | tf_op jit(solution)/shard_map/all_to_all | solution.py:239
  (70 shorter events, 32.5 us)
Async XLA Ops:
  0.0 74.4 %copy-start = (f32[8,32]{1,0:T(8,128)S(1)}, f32[8,32]{1,0:T(8,128)}, u32[]{:S(2)}) copy-start(f32[8,32]{1,0:T(8,128)} %param.13) | copy-start | bytes 3076
  2.6 9.3 %collective-permute-start = (bf16[8,64,256]{2,1,0:T(8,128)(2,1)S(1)}, bf16[8,64,256]{2,1,0:T(8,128)(2,1)S(1)}, u32[]{:S(2)}, u32[]{:S(2)}) collective-permute-start(bf16[8,64,256]{2,1,0:T(8,128)(2,1)S(1)} %and_select_fusion), channel_id=1, source_target_pairs={{0,2},{1,3},{2,0},{3,1},{4,6},{5,7},{6,4},{7,5},{8,10},{9,11},{10,... | collective-permute-start | bytes 786440 | tf_op jit(solution)/shard_map/ppermute | solution.py:199
  12.8 49.4 %copy-start.4 = (bf16[8,64,256]{2,1,0:T(8,128)(2,1)S(1)}, bf16[8,64,256]{2,1,0:T(8,128)(2,1)}, u32[]{:S(2)}) copy-start(bf16[8,64,256]{2,1,0:T(8,128)(2,1)} %param.10) | copy-start | bytes 786436
  12.8 13.1 %collective-permute-start.4 = (bf16[8,128,256]{2,1,0:T(8,128)(2,1)S(1)}, bf16[8,128,256]{2,1,0:T(8,128)(2,1)S(1)}, u32[]{:S(2)}, u32[]{:S(2)}) collective-permute-start(bf16[8,128,256]{2,1,0:T(8,128)(2,1)S(1)} %get-tuple-element.13), channel_id=1, source_target_pairs={{0,8},{8,16},{16,24},{24,28},{28,20},{20,12},{12,4},{4,0},{1,9},{9... | collective-permute-start | bytes 1572872 | tf_op jit(solution)/shard_map/ppermute | solution.py:171
  14.7 12.8 %collective-permute-start.1 = (bf16[8,128,256]{2,1,0:T(8,128)(2,1)S(1)}, bf16[8,128,256]{2,1,0:T(8,128)(2,1)S(1)}, u32[]{:S(2)}, u32[]{:S(2)}) collective-permute-start(bf16[8,128,256]{2,1,0:T(8,128)(2,1)S(1)} %get-tuple-element.13), channel_id=1, source_target_pairs={{8,0},{16,8},{24,16},{28,24},{20,28},{12,20},{4,12},{0,4},{9,1},{1... | collective-permute-start | bytes 1572872 | tf_op jit(solution)/shard_map/ppermute | solution.py:172
  25.9 12.2 %collective-permute-start.5 = (bf16[8,128,256]{2,1,0:T(8,128)(2,1)S(1)}, bf16[8,128,256]{2,1,0:T(8,128)(2,1)S(1)}, u32[]{:S(2)}, u32[]{:S(2)}) collective-permute-start(bf16[8,128,256]{2,1,0:T(8,128)(2,1)S(1)} %collective-permute-done.4), channel_id=1, source_target_pairs={{0,8},{8,16},{16,24},{24,28},{28,20},{20,12},{12,4},{4,0},{1,9},{9... | collective-permute-start | bytes 1572872 | tf_op jit(solution)/shard_map/ppermute | solution.py:171
  27.5 12.1 %collective-permute-start.2 = (bf16[8,128,256]{2,1,0:T(8,128)(2,1)S(1)}, bf16[8,128,256]{2,1,0:T(8,128)(2,1)S(1)}, u32[]{:S(2)}, u32[]{:S(2)}) collective-permute-start(bf16[8,128,256]{2,1,0:T(8,128)(2,1)S(1)} %collective-permute-done.1), channel_id=1, source_target_pairs={{8,0},{16,8},{24,16},{28,24},{20,28},{12,20},{4,12},{0,4},{9,1},{1... | collective-permute-start | bytes 1572872 | tf_op jit(solution)/shard_map/ppermute | solution.py:172
  38.2 12.0 %collective-permute-start.6 = (bf16[8,128,256]{2,1,0:T(8,128)(2,1)S(1)}, bf16[8,128,256]{2,1,0:T(8,128)(2,1)S(1)}, u32[]{:S(2)}, u32[]{:S(2)}) collective-permute-start(bf16[8,128,256]{2,1,0:T(8,128)(2,1)S(1)} %collective-permute-done.5), channel_id=1, source_target_pairs={{0,8},{8,16},{16,24},{24,28},{28,20},{20,12},{12,4},{4,0},{1,9},{9... | collective-permute-start | bytes 1572872 | tf_op jit(solution)/shard_map/ppermute | solution.py:171
  39.6 12.9 %collective-permute-start.3 = (bf16[8,128,256]{2,1,0:T(8,128)(2,1)S(1)}, bf16[8,128,256]{2,1,0:T(8,128)(2,1)S(1)}, u32[]{:S(2)}, u32[]{:S(2)}) collective-permute-start(bf16[8,128,256]{2,1,0:T(8,128)(2,1)S(1)} %collective-permute-done.2), channel_id=1, source_target_pairs={{8,0},{16,8},{24,16},{28,24},{20,28},{12,20},{4,12},{0,4},{9,1},{1... | collective-permute-start | bytes 1572872 | tf_op jit(solution)/shard_map/ppermute | solution.py:172
  50.2 6.4 %collective-permute-start.7 = (bf16[4,128,256]{2,1,0:T(8,128)(2,1)S(1)}, bf16[4,128,256]{2,1,0:T(8,128)(2,1)S(1)}, u32[]{:S(2)}, u32[]{:S(2)}) collective-permute-start(bf16[4,128,256]{2,1,0:T(8,128)(2,1)S(1)} %slice.40), channel_id=1, source_target_pairs={{0,8},{8,16},{16,24},{24,28},{28,20},{20,12},{12,4},{4,0},{1,9},{9... | collective-permute-start | bytes 786440 | tf_op jit(solution)/shard_map/ppermute | solution.py:175
  52.5 6.4 %collective-permute-start.8 = (bf16[4,128,256]{2,1,0:T(8,128)(2,1)S(1)}, bf16[4,128,256]{2,1,0:T(8,128)(2,1)S(1)}, u32[]{:S(2)}, u32[]{:S(2)}) collective-permute-start(bf16[4,128,256]{2,1,0:T(8,128)(2,1)S(1)} %slice.41), channel_id=1, source_target_pairs={{8,0},{16,8},{24,16},{28,24},{20,28},{12,20},{4,12},{0,4},{9,1},{1... | collective-permute-start | bytes 786440 | tf_op jit(solution)/shard_map/ppermute | solution.py:176
  62.2 50.1 %collective-permute-start.9 = (bf16[64,128,256]{2,1,0:T(8,128)(2,1)}, bf16[64,128,256]{2,1,0:T(8,128)(2,1)}, u32[]{:S(2)}, u32[]{:S(2)}) collective-permute-start(bf16[64,128,256]{2,1,0:T(8,128)(2,1)} %constant_dynamic-update-slice_fusion.refs_0_.refs_1_.refs_2_.refs_3_.refs_17_), channel_id=1, source_target_pairs={{0,1},{1,0},{2,3},{3,2},{4,5},{5,4},{6,7},{7,6},{8,9},{9,8},{10,11... | collective-permute-start | bytes 12582920 | tf_op jit(solution)/shard_map/ppermute | solution.py:199
  65.6 19.7 %copy-start.5 = (s32[8]{0:T(128)S(1)}, s32[8]{0:T(128)}, u32[]{:S(2)}) copy-start(s32[8]{0:T(128)} %param.8) | copy-start | bytes 100
  65.6 46.2 %collective-permute-start.10 = (bf16[2,33,64,256]{3,2,1,0:T(8,128)(2,1)}, bf16[2,33,64,256]{3,2,1,0:T(8,128)(2,1)S(1)}, u32[]{:S(2)}, u32[]{:S(2)}) collective-permute-start(bf16[2,33,64,256]{3,2,1,0:T(8,128)(2,1)} %pad_maximum_fusion), channel_id=1, source_target_pairs={{0,1},{1,0},{2,3},{3,2},{4,5},{5,4},{6,7},{7,6},{8,9},{9,8},{10,11... | collective-permute-start | bytes 6488072 | tf_op jit(solution)/shard_map/ppermute | solution.py:199
  70.1 15.1 %collective-permute-start.15 = (bf16[2,8,64,256]{3,2,1,0:T(8,128)(2,1)}, bf16[2,8,64,256]{3,2,1,0:T(8,128)(2,1)}, u32[]{:S(2)}, u32[]{:S(2)}) collective-permute-start(bf16[2,8,64,256]{3,2,1,0:T(8,128)(2,1)} %get-tuple-element.8), channel_id=1, source_target_pairs={{0,2},{1,3},{2,0},{3,1},{4,6},{5,7},{6,4},{7,5},{8,10},{9,11},{10,... | collective-permute-start | bytes 1572872 | tf_op jit(solution)/shard_map/ppermute | solution.py:199
  72.5 25.3 %collective-permute-start.17 = (bf16[2,9,64,256]{3,2,1,0:T(8,128)(2,1)}, bf16[2,9,64,256]{3,2,1,0:T(8,128)(2,1)S(1)}, u32[]{:S(2)}, u32[]{:S(2)}) collective-permute-start(bf16[2,9,64,256]{3,2,1,0:T(8,128)(2,1)} %pad_maximum_fusion.1), channel_id=1, source_target_pairs={{0,2},{1,3},{2,0},{3,1},{4,6},{5,7},{6,4},{7,5},{8,10},{9,11},{10,... | collective-permute-start | bytes 1769480 | tf_op jit(solution)/shard_map/ppermute | solution.py:199
  73.9 35.6 %collective-permute-start.18 = (bf16[2,9,64,256]{3,2,1,0:T(8,128)(2,1)}, bf16[2,9,64,256]{3,2,1,0:T(8,128)(2,1)S(1)}, u32[]{:S(2)}, u32[]{:S(2)}) collective-permute-start(bf16[2,9,64,256]{3,2,1,0:T(8,128)(2,1)} %pad_maximum_fusion.2), channel_id=1, source_target_pairs={{0,3},{1,2},{2,1},{3,0},{4,7},{5,6},{6,5},{7,4},{8,11},{9,10},{10,... | collective-permute-start | bytes 1769480 | tf_op jit(solution)/shard_map/ppermute | solution.py:199
  85.2 35.5 %collective-permute-start.16 = (bf16[2,8,64,256]{3,2,1,0:T(8,128)(2,1)}, bf16[2,8,64,256]{3,2,1,0:T(8,128)(2,1)}, u32[]{:S(2)}, u32[]{:S(2)}) collective-permute-start(bf16[2,8,64,256]{3,2,1,0:T(8,128)(2,1)} %get-tuple-element.7), channel_id=1, source_target_pairs={{0,3},{1,2},{2,1},{3,0},{4,7},{5,6},{6,5},{7,4},{8,11},{9,10},{10,... | collective-permute-start | bytes 1572872 | tf_op jit(solution)/shard_map/ppermute | solution.py:199
  97.8 15.2 %copy-start.2 = (bf16[2,9,64,256]{3,2,1,0:T(8,128)(2,1)}, bf16[2,9,64,256]{3,2,1,0:T(8,128)(2,1)S(1)}, u32[]{:S(2)}) copy-start(bf16[2,9,64,256]{3,2,1,0:T(8,128)(2,1)S(1)} %collective-permute-done.17.refs_10_.refs_14_) | copy-start | bytes 1769476
  97.8 35.2 %collective-permute-start.13 = (bf16[2,8,64,256]{3,2,1,0:T(8,128)(2,1)}, bf16[2,8,64,256]{3,2,1,0:T(8,128)(2,1)}, u32[]{:S(2)}, u32[]{:S(2)}) collective-permute-start(bf16[2,8,64,256]{3,2,1,0:T(8,128)(2,1)} %get-tuple-element.10), channel_id=1, source_target_pairs={{0,2},{1,3},{2,0},{3,1},{4,6},{5,7},{6,4},{7,5},{8,10},{9,11},{10,... | collective-permute-start | bytes 1572872 | tf_op jit(solution)/shard_map/ppermute | solution.py:199
  109.5 3.4 %copy-start.3 = (bf16[2,9,64,256]{3,2,1,0:T(8,128)(2,1)}, bf16[2,9,64,256]{3,2,1,0:T(8,128)(2,1)S(1)}, u32[]{:S(2)}) copy-start(bf16[2,9,64,256]{3,2,1,0:T(8,128)(2,1)S(1)} %collective-permute-done.18.refs_11_.refs_15_) | copy-start | bytes 1769476
  109.5 33.7 %collective-permute-start.14 = (bf16[2,8,64,256]{3,2,1,0:T(8,128)(2,1)}, bf16[2,8,64,256]{3,2,1,0:T(8,128)(2,1)}, u32[]{:S(2)}, u32[]{:S(2)}) collective-permute-start(bf16[2,8,64,256]{3,2,1,0:T(8,128)(2,1)} %get-tuple-element.9), channel_id=1, source_target_pairs={{0,3},{1,2},{2,1},{3,0},{4,7},{5,6},{6,5},{7,4},{8,11},{9,10},{10,... | collective-permute-start | bytes 1572872 | tf_op jit(solution)/shard_map/ppermute | solution.py:199
  111.7 43.7 %collective-permute-start.11 = (bf16[2,8,64,256]{3,2,1,0:T(8,128)(2,1)}, bf16[2,8,64,256]{3,2,1,0:T(8,128)(2,1)}, u32[]{:S(2)}, u32[]{:S(2)}) collective-permute-start(bf16[2,8,64,256]{3,2,1,0:T(8,128)(2,1)} %get-tuple-element.12), channel_id=1, source_target_pairs={{0,2},{1,3},{2,0},{3,1},{4,6},{5,7},{6,4},{7,5},{8,10},{9,11},{10,... | collective-permute-start | bytes 1572872 | tf_op jit(solution)/shard_map/ppermute | solution.py:199
  112.3 52.4 %collective-permute-start.12 = (bf16[2,8,64,256]{3,2,1,0:T(8,128)(2,1)}, bf16[2,8,64,256]{3,2,1,0:T(8,128)(2,1)}, u32[]{:S(2)}, u32[]{:S(2)}) collective-permute-start(bf16[2,8,64,256]{3,2,1,0:T(8,128)(2,1)} %get-tuple-element.11), channel_id=1, source_target_pairs={{0,3},{1,2},{2,1},{3,0},{4,7},{5,6},{6,5},{7,4},{8,11},{9,10},{10,... | collective-permute-start | bytes 1572872 | tf_op jit(solution)/shard_map/ppermute | solution.py:199
  (1 other events, 1.4 us)

commit v2 on v0

v2 whole, which is shorter than its diff:
```python
import functools
import jax
import jax.numpy as jnp
from jax import lax
from jax.experimental import pallas as pl
from jax.experimental.pallas import tpu as pltpu
from jax.sharding import PartitionSpec as P

CHUNKS = (24, 29)
RING_MAX = 8


def coupled_kernel(
    first, last, size, start, stride, offsets,
    slot_ref, weight_ref, info_ref, near, far, own, *refs,
):
    refs = list(refs)
    ways = len(offsets) + 1
    own_pairs = (info_ref.shape[0] - 1 - ways) // 2
    got = [refs.pop(0) for _ in range(ways - 1)]
    if first:
        exch, fock = refs.pop(0), refs.pop(0)
    else:
        acc = refs.pop(0)
    outs = [refs.pop(0) for _ in range(ways if last else 1)]
    left, right, proj, left_sem, right_sem = (refs.pop(0) for _ in range(5))
    group, share, width = right.shape[1], right.shape[3], right.shape[4]
    order = list(range(0, ways, 2)) + list(range(1, ways, 2))
    rounds = size // group
    column = info_ref[0]

    def block(k):
        return info_ref[1 + 2 * own_pairs + k]

    def fetch_partner(slot, place, sem):
        pltpu.make_async_copy(near.at[slot], place.at[0], sem).start()
        pltpu.make_async_copy(far.at[slot], place.at[1], sem).start()

    def fetch(r, _):
        m, q = lax.div(r, rounds), lax.rem(r, rounds) * group
        for g in range(group):
            fetch_partner(slot_ref[m * stride + start + q + g], left.at[r, g], left_sem.at[r])
        pltpu.make_async_copy(
            own.at[column * own_pairs + m, pl.ds(start + q, group)],
            right.at[r, :, block(0)], right_sem.at[r]).start()
        for k in range(1, ways):
            pltpu.make_async_copy(
                got[k - 1].at[m, pl.ds(offsets[k - 1] + q, group)],
                right.at[r, :, block(k)], right_sem.at[r]).start()
        return 0

    if first:
        base, mine, whole, base_sem, mine_sem, whole_sem = refs
        for m in range(own_pairs):
            pltpu.make_async_copy(
                fock.at[column * own_pairs + m], whole.at[m], whole_sem.at[m]).start()
            fetch_partner(info_ref[1 + own_pairs + m], mine.at[m], mine_sem.at[m])
            pltpu.make_async_copy(
                exch.at[column * own_pairs + m], base.at[m, block(0)], base_sem.at[m]).start()
            for k in range(1, ways):
                pltpu.make_async_copy(
                    got[k - 1].at[m, got[k - 1].shape[1] - 1], base.at[m, block(k)], base_sem.at[m]
                ).start()
    else:
        whole, whole_sem = refs
        for m in range(own_pairs):
            pltpu.make_async_copy(acc.at[m], whole.at[m], whole_sem.at[m]).start()
    lax.fori_loop(0, own_pairs * rounds, fetch, 0)

    def ready(ref, sem, i):
        pltpu.make_async_copy(ref.at[i], ref.at[i], sem.at[i]).wait()

    def arranged(rows, g):
        for n, k in enumerate(order):
            proj[g, block(k)] = rows[n * share:(n + 1) * share]

    for m in range(own_pairs):
        ready(whole, whole_sem, m)
        total = whole if last else outs[0]
        if first:
            ready(mine, mine_sem, m)
            ready(base, base_sem, m)
            arranged(mine[m].reshape(width, width), 0)
            diagonal = whole[m]
            block_own = proj[0].reshape(width, width)
            sums = base[m].reshape(width, width).astype(jnp.float32)
            sums = sums + jnp.dot(diagonal, block_own, preferred_element_type=jnp.float32)
            total[m] = sums + jnp.dot(block_own, diagonal, preferred_element_type=jnp.float32)
        elif not last:
            total[m] = whole[m]

        def body(n, _):
            r = m * rounds + n
            ready(left, left_sem, r)
            ready(right, right_sem, r)
            for g in range(group):
                prod = jnp.dot(
                    left[r, g].reshape(width, width), right[r, g].reshape(width, width),
                    preferred_element_type=jnp.float32)
                arranged(prod.astype(jnp.bfloat16), g)
            added = None
            for g in range(group):
                term = lax.dot_general(
                    right[r, g].reshape(width, width), proj[g].reshape(width, width),
                    (((0,), (0,)), ((), ())), preferred_element_type=jnp.float32)
                term = weight_ref[m * stride + start + n * group + g] * term
                added = term if added is None else added + term
            total[m] = total[m] + added
            return 0

        lax.fori_loop(0, rounds, body, 0)
        if last:
            count = info_ref[1 + m]
            row = lax.broadcasted_iota(jnp.int32, (width, width), 0)
            col = lax.broadcasted_iota(jnp.int32, (width, width), 1)
            keep = (row < count) & (col < count)
            total[m] = jnp.where(keep, total[m], 0.0)
            for k in range(ways):
                rows = pl.ds(pl.multiple_of(block(k) * share, share), share)
                outs[k][m] = total[m, rows, :].astype(jnp.bfloat16)


def run_chunk(
    start, size, first, last, near, far, own_pieces, got, slots, weights, info, acc, exch, fock
):
    own_pairs = got[0][0].shape[0]
    ways = len(got) + 1
    width = near.shape[2]
    share = own_pieces.shape[2]
    units = own_pairs * size
    anywhere = pl.BlockSpec(memory_space=pl.ANY)
    operands = [near, far, own_pieces] + [piece for piece, _ in got]
    operands += [exch, fock] if first else [acc]
    inside = pl.BlockSpec(memory_space=pltpu.VMEM)
    if last:
        out_shape = [jax.ShapeDtypeStruct((own_pairs, share, width), jnp.bfloat16)] * ways
        out_specs = [inside] * ways
    else:
        out_shape = jax.ShapeDtypeStruct((own_pairs, width, width), jnp.float32)
        out_specs = inside
    group = max(g for g in (1, 2, 3, 4, 5) if size % g == 0)
    rounds = units // group
    scratch = [
        pltpu.VMEM((rounds, group, 2, width // 2, width), jnp.bfloat16),
        pltpu.VMEM((rounds, group, ways, share, width), jnp.bfloat16),
        pltpu.VMEM((group, ways, share, width), jnp.bfloat16),
        pltpu.SemaphoreType.DMA((rounds,)),
        pltpu.SemaphoreType.DMA((rounds,)),
    ]
    pair_sems = pltpu.SemaphoreType.DMA((own_pairs,))
    if first:
        scratch += [
            pltpu.VMEM((own_pairs, ways, share, width), jnp.bfloat16),
            pltpu.VMEM((own_pairs, 2, width // 2, width), jnp.bfloat16),
            pltpu.VMEM((own_pairs, width, width), jnp.bfloat16),
            pair_sems, pair_sems, pair_sems,
        ]
    else:
        scratch += [pltpu.VMEM((own_pairs, width, width), jnp.float32), pair_sems]
    stride = slots.shape[0] // own_pairs
    return pl.pallas_call(
        functools.partial(
            coupled_kernel, first, last, size, start, stride, tuple(o for _, o in got)),
        out_shape=out_shape,
        grid_spec=pltpu.PrefetchScalarGridSpec(
            num_scalar_prefetch=3,
            grid=(),
            in_specs=[anywhere] * len(operands),
            out_specs=out_specs,
            scratch_shapes=scratch,
        ),
        cost_estimate=pl.CostEstimate(
            flops=units * 4 * width**3, bytes_accessed=units * 4 * width**2, transcendentals=0),
        name="coupled",
    )(slots, weights, info, *operands)


def gather_pairs(half, count):
    me = lax.axis_index("pairs")
    if count > RING_MAX or count % 2:
        return lax.all_gather(half, "pairs", axis=0, tiled=True), lambda block: block
    order = list(range(0, count, 2)) + list(range(count - 1, 0, -2))
    ahead = [(order[i], order[(i + 1) % count]) for i in range(count)]
    behind = [(b, a) for a, b in ahead]
    mid = half.shape[0] // 2
    forward = backward = half
    from_ahead, from_behind = [], []
    for _ in range(1, count // 2):
        forward = lax.ppermute(forward, "pairs", ahead)
        backward = lax.ppermute(backward, "pairs", behind)
        from_behind.append(forward)
        from_ahead.append(backward)
    low = lax.ppermute(forward[:mid], "pairs", ahead)
    high = lax.ppermute(backward[mid:], "pairs", behind)
    whole = jnp.concatenate([half] + from_ahead + [low, high] + from_behind[::-1], axis=0)

    def place_of(block):
        return jnp.where(block % 2 == 0, block // 2, count - 1 - block // 2)

    return whole, lambda block: (place_of(block) - place_of(me) + count) % count


def chunk_bounds(length):
    cuts = [0] + [length * c // 32 for c in CHUNKS] + [length]
    return list(zip(cuts, cuts[1:]))


def shards(
    columns, amplitudes, pno_counts, fock_blocks, exchange_blocks, intersections, partners, couplings
):
    local_pairs, share, width = amplitudes.shape
    ways, count = columns, lax.axis_size("pairs")
    slots_per_pair = partners.shape[1]
    own_pairs = local_pairs // ways
    column = lax.axis_index("cols")

    def swap(array, k):
        return lax.ppermute(array, "cols", [(c, c ^ k) for c in range(ways)])

    col_keep = jnp.arange(width, dtype=jnp.int32)[None, :] < pno_counts[:, None]

    def masked(array, k):
        row = (column ^ k) * share + jnp.arange(share, dtype=jnp.int32)
        keep = (row[None, :] < pno_counts[:, None])[:, :, None] & col_keep[:, None, :]
        return jnp.where(keep, array, jnp.zeros_like(array))

    parts = [masked(amplitudes, 0)]
    parts += [masked(swap(amplitudes, k), k) for k in range(2, ways, 2)]
    half = jnp.concatenate(parts, axis=1)
    bounds = chunk_bounds(slots_per_pair)

    def moved(k, start, stop):
        begin = (column ^ k) * own_pairs
        piece = lax.dynamic_slice(
            intersections, (begin, start, 0, 0), (own_pairs, stop - start, share, width))
        if start == 0:
            extra = lax.dynamic_slice_in_dim(exchange_blocks, begin, own_pairs, 0)
            piece = jnp.concatenate([piece, extra[:, None]], axis=1)
        return swap(piece, k)

    beside = moved(1, 0, slots_per_pair)
    got = []
    for start, stop in bounds:
        got.append([(beside, start)] + [
            (moved(k, start, stop), 0) for k in range(2, ways)])

    near, place = gather_pairs(half, count)
    far = swap(near, 1)

    begin = column * own_pairs
    own_partners = lax.dynamic_slice_in_dim(partners, begin, own_pairs, 0)
    weights = lax.dynamic_slice_in_dim(couplings, begin, own_pairs, 0)
    slots = place(own_partners // local_pairs) * local_pairs + own_partners % local_pairs
    own_counts = lax.dynamic_slice_in_dim(pno_counts, begin, own_pairs, 0)
    own_slots = place(lax.axis_index("pairs")) * local_pairs + begin + jnp.arange(own_pairs, dtype=jnp.int32)
    blocks = column ^ jnp.arange(ways, dtype=jnp.int32)
    info = jnp.concatenate([column[None].astype(jnp.int32), own_counts, own_slots, blocks])

    acc = None
    for n, (start, stop) in enumerate(bounds):
        acc = run_chunk(
            start, stop - start, n == 0, n == len(bounds) - 1, near, far, intersections,
            got[n], slots.reshape(-1), weights.reshape(-1), info, acc, exchange_blocks, fock_blocks)
    arrived = [acc[0]] + [swap(acc[k], k) for k in range(1, ways)]
    spots = blocks[:, None, None, None]
    shared = arrived[0][None]
    for k in range(1, ways):
        shared = jnp.where(spots == k, arrived[k][None], shared)
    return shared.reshape(local_pairs, share, width)


def solution(mesh):
    in_specs = (
        P("pairs", "cols", None),
        P("pairs"),
        P("pairs", None, None),
        P("pairs", "cols", None),
        P("pairs", None, "cols", None),
        P("pairs", None),
        P("pairs", None),
    )
    out_specs = P("pairs", "cols", None)
    ways = mesh.shape["cols"]
    body = functools.partial(shards, ways)
    return jax.shard_map(body, mesh=mesh, in_specs=in_specs, out_specs=out_specs, check_vma=False)
```

time: 407 us -> 176 us (0.43)
  waiting for transfers between devices: 271 us -> 109 us
  matrix products: 105 us -> 0 us
  Pallas kernels: 0 us -> 19.4 us
  starting transfers between devices: 0.08 us -> 19.2 us
  between operations: 13.2 us -> 0.15 us
  other arithmetic: 3.37 us -> 10.9 us
    all_gather x2 -> x0, waiting for transfers between devices: 239 us -> none  [the longest x1 189 us: shards(): lax.all_gather(intersections, 'cols', axis=2, tiled=True)]
    ppermute x0 -> x20, waiting for transfers between devices: none -> 109 us  [the longest x12 74.7 us: swap(): return lax.ppermute(array, 'cols', [(c, c ^ k) for c in range(ways)])]
    dot_general x35 -> x0, matrix products: 105 us -> none  [the longest x32 64.2 us: shards(): jnp.einsum('pcd,pca->pda', intersections[:, slot_index], projected[:, slo...]
    reduce_scatter x1 -> x0, waiting for transfers between devices: 31.3 us -> none  [shards(): lax.psum_scatter(partial_value, 'cols', scatter_dimension=1, tiled=True)]
    pallas_call x0 -> x3, Pallas kernels: none -> 19.4 us  [run_chunk(): pl.pallas_call(functools.partial(coupled_kernel, first, last, size, start...]
    ppermute x0 -> x20, starting transfers between devices: none -> 19.2 us  [the longest x12 11 us: swap(): return lax.ppermute(array, 'cols', [(c, c ^ k) for c in range(ways)])]
    gather x1 -> x0, local copies, waits for them, and re-layouts: 12.4 us -> none  [shards(): picked = piece[jnp.clip(linear, 0, piece.shape[0] - 1)]]
    dynamic_slice x0 -> x6, local copies, waits for them, and re-layouts: none -> 7.09 us  [the longest x4 7.01 us: moved(): lax.dynamic_slice(intersections, (begin, start, 0, 0), (own_pairs, stop -...]
  transfers between devices with their start and end apart: 3 -> 20, of which waited for: 3 -> 13; matrix products, arithmetic and copies ran while one was open for 3% -> 11% of each run, Pallas kernels for 0% -> 9%
where the time goes in v2:
time: 176 us; the launch traced here: 175 us
  waiting for transfers between devices  109 us (62%)
  Pallas kernels  19.4 us (11%)
  starting transfers between devices  19.2 us (11%)
  local copies, waits for them, and re-layouts  16.2 us (9%)
  other arithmetic  10.9 us (6%)
    ppermute x12, waiting for transfers between devices, swap(): return lax.ppermute(array, 'cols', [(c, c ^ k) for c in range(ways)])  74.7 us
    ppermute x3, waiting for transfers between devices, gather_pairs(): forward = lax.ppermute(forward, 'pairs', ahead)  31.2 us
    pallas_call x3, Pallas kernels, run_chunk(): pl.pallas_call(functools.partial(coupled_kernel, first, last, size, start...  19.4 us
    ppermute x12, starting transfers between devices, swap(): return lax.ppermute(array, 'cols', [(c, c ^ k) for c in range(ways)])  11 us
    dynamic_slice x4, local copies, waits for them, and re-layouts, moved(): lax.dynamic_slice(intersections, (begin, start, 0, 0), (own_pairs, stop -...  7.01 us
    unnamed x19, local copies, waits for them, and re-layouts  6.46 us
    ppermute x3, starting transfers between devices, gather_pairs(): forward = lax.ppermute(forward, 'pairs', ahead)  4.78 us
    concatenate x3, other arithmetic, moved(): piece = jnp.concatenate([piece, extra[:, None]], axis=1)  4.22 us
  transfers between devices with their start and end apart: 20, of which 13 were waited for; matrix products, arithmetic and copies ran while one was open for 11% of the time, Pallas kernels for 9%

profile of v2, /device:TPU:0, one launch (start us, length us, event | category | flops | bytes accessed | tf_op | source)
XLA Modules:
  0.0 175.2 jit_solution(4910230923065272054)
XLA Ops:
  0.0 3.0 %collective-permute-start = (bf16[8,64,256]{2,1,0:T(8,128)(2,1)}, bf16[8,64,256]{2,1,0:T(8,128)(2,1)S(1)}, u32[]{:S(2)}, u32[]{:S(2)}) collective-permute-start(bf16[8,64,256]{2,1,0:T(8,128)(2,1)} %param.7), channel_id=1, source_target_pairs={{0,2},{1,3},{2,0},{3,1},{4,6},{5,7},{6,4},{7,5},{8,10},{9,11},{10,... | collective-permute-start | bytes 786440 | tf_op jit(solution)/shard_map/ppermute | solution.py:218
  4.4 5.1 %collective-permute-done = bf16[8,64,256]{2,1,0:T(8,128)(2,1)S(1)} collective-permute-done((bf16[8,64,256]{2,1,0:T(8,128)(2,1)}, bf16[8,64,256]{2,1,0:T(8,128)(2,1)S(1)}, u32[]{:S(2)}, u32[]{:S(2)}) %collective-permute-start) | collective-permute-done | bytes 262176 | tf_op jit(solution)/shard_map/ppermute | solution.py:218
  11.6 1.8 %collective-permute-start.4 = (bf16[8,128,256]{2,1,0:T(8,128)(2,1)S(1)}, bf16[8,128,256]{2,1,0:T(8,128)(2,1)S(1)}, u32[]{:S(2)}, u32[]{:S(2)}) collective-permute-start(bf16[8,128,256]{2,1,0:T(8,128)(2,1)S(1)} %get-tuple-element.19), channel_id=1, source_target_pairs={{0,8},{8,16},{16,24},{24,28},{28,20},{20,12},{12,4},{4,0},{1,9},{9... | collective-permute-start | bytes 1572872 | tf_op jit(solution)/shard_map/ppermute | solution.py:189
  13.6 11.1 %collective-permute-done.4 = bf16[8,128,256]{2,1,0:T(8,128)(2,1)S(1)} collective-permute-done((bf16[8,128,256]{2,1,0:T(8,128)(2,1)S(1)}, bf16[8,128,256]{2,1,0:T(8,128)(2,1)S(1)}, u32[]{:S(2)}, u32[]{:S(2)}) %collective-permute-start.4) | collective-permute-done | bytes 524320 | tf_op jit(solution)/shard_map/ppermute | solution.py:189
  24.7 1.5 collective-permute-start.5
  26.7 10.2 %collective-permute-done.5 = bf16[8,128,256]{2,1,0:T(8,128)(2,1)S(1)} collective-permute-done((bf16[8,128,256]{2,1,0:T(8,128)(2,1)S(1)}, bf16[8,128,256]{2,1,0:T(8,128)(2,1)S(1)}, u32[]{:S(2)}, u32[]{:S(2)}) %collective-permute-start.5) | collective-permute-done | bytes 524320 | tf_op jit(solution)/shard_map/ppermute | solution.py:189
  39.0 10.0 %collective-permute-done.6 = bf16[8,128,256]{2,1,0:T(8,128)(2,1)S(1)} collective-permute-done((bf16[8,128,256]{2,1,0:T(8,128)(2,1)S(1)}, bf16[8,128,256]{2,1,0:T(8,128)(2,1)S(1)}, u32[]{:S(2)}, u32[]{:S(2)}) %collective-permute-start.6) | collective-permute-done | bytes 524320 | tf_op jit(solution)/shard_map/ppermute | solution.py:189
  53.6 1.8 %collective-permute-done.7 = bf16[4,128,256]{2,1,0:T(8,128)(2,1)S(1)} collective-permute-done((bf16[4,128,256]{2,1,0:T(8,128)(2,1)S(1)}, bf16[4,128,256]{2,1,0:T(8,128)(2,1)S(1)}, u32[]{:S(2)}, u32[]{:S(2)}) %collective-permute-start.7) | collective-permute-done | bytes 262176 | tf_op jit(solution)/shard_map/ppermute | solution.py:193
  56.1 1.6 collective-permute-done.8
  61.1 1.8 %constant_dynamic-slice_fusion.6 = bf16[2,32,64,256]{3,2,1,0:T(8,128)(2,1)S(1)} fusion(bf16[8,32,64,256]{3,2,1,0:T(8,128)(2,1)} %own.5, s32[]{:T(128)S(6)} %select_n.107), kind=kLoop, calls=%fused_computation.28 | loop fusion | bytes 4194308 | tf_op jit(solution)/shard_map/dynamic_slice | solution.py:234
  62.9 1.6 pad_maximum_fusion
  65.0 2.3 %constant_dynamic-slice_fusion = (bf16[2,24,64,256]{3,2,1,0:T(8,128)(2,1)S(1)}, bf16[2,24,64,256]{3,2,1,0:T(8,128)(2,1)S(1)}) fusion(bf16[8,32,64,256]{3,2,1,0:T(8,128)(2,1)} %own.5, s32[]{:T(128)S(6)} %select_n.109, s32[]{:T(128)S(6)} %select_n.108), kind=kLoop, calls=%fused_computation.22 | loop fusion | bytes 6291464 | tf_op jit(solution)/shard_map/dynamic_slice | solution.py:234
  74.8 1.8 %constant_dynamic-slice_fusion.4 = (bf16[2,3,64,256]{3,2,1,0:T(8,128)(2,1)}, bf16[2,3,64,256]{3,2,1,0:T(8,128)(2,1)}) fusion(bf16[8,32,64,256]{3,2,1,0:T(8,128)(2,1)} %own.5, s32[]{:T(128)S(6)} %select_n.109, s32[]{:T(128)S(6)} %select_n.108), kind=kLoop, calls=%fused_computation.26 | loop fusion | bytes 786440 | tf_op jit(solution)/shard_map/dynamic_slice | solution.py:234
  76.6 31.0 %collective-permute-done.15.refs_1_ = bf16[2,25,64,256]{3,2,1,0:T(8,128)(2,1)} collective-permute-done((bf16[2,25,64,256]{3,2,1,0:T(8,128)(2,1)}, bf16[2,25,64,256]{3,2,1,0:T(8,128)(2,1)}, u32[]{:S(2)}, u32[]{:S(2)}) %collective-permute-start.15) | collective-permute-done | bytes 1638432 | tf_op jit(solution)/shard_map/ppermute | solution.py:218
  109.9 31.8 %collective-permute-done.16.refs_2_ = bf16[2,25,64,256]{3,2,1,0:T(8,128)(2,1)} collective-permute-done((bf16[2,25,64,256]{3,2,1,0:T(8,128)(2,1)}, bf16[2,25,64,256]{3,2,1,0:T(8,128)(2,1)}, u32[]{:S(2)}, u32[]{:S(2)}) %collective-permute-start.16) | collective-permute-done | bytes 1638432 | tf_op jit(solution)/shard_map/ppermute | solution.py:218
  142.3 1.6 collective-permute-start.12
  143.9 11.1 %coupled.3.refs_3_ = f32[2,256,256]{2,1,0:T(8,128)} custom-call(s32[64]{0:T(128)} %reshape.113.slot_ref, f32[64]{0:T(128)} %reshape.114.weight_ref, s32[9]{0:T(128)} %pad_add_fusion.info_ref, bf16[64,128,256]{2,1,0:T(8,128)(2,1)} %constant_dynamic-update-slice_fusion.near, bf16[64,128,256]{2,1,0:T(8,128)(2,1)} %collective-permute-done.9.far, ...), custom_call_target="tpu_custom_call" | custom-call | flops 3221225472 | bytes 12582912 | tf_op jit(solution)/shard_map/coupled/pallas_call | solution.py:161
  156.4 4.5 %coupled.4.refs_3_ = f32[2,256,256]{2,1,0:T(8,128)} custom-call(s32[64]{0:T(128)} %reshape.113.slot_ref, f32[64]{0:T(128)} %reshape.114.weight_ref, s32[9]{0:T(128)} %pad_add_fusion.info_ref, bf16[64,128,256]{2,1,0:T(8,128)(2,1)} %constant_dynamic-update-slice_fusion.near, bf16[64,128,256]{2,1,0:T(8,128)(2,1)} %collective-permute-done.9.far, ...), custom_call_target="tpu_custom_call" | custom-call | flops 671088640 | bytes 2621440 | tf_op jit(solution)/shard_map/coupled/pallas_call | solution.py:161
  161.0 2.3 %collective-permute-done.12.refs_2_ = bf16[2,3,64,256]{3,2,1,0:T(8,128)(2,1)} collective-permute-done((bf16[2,3,64,256]{3,2,1,0:T(8,128)(2,1)}, bf16[2,3,64,256]{3,2,1,0:T(8,128)(2,1)}, u32[]{:S(2)}, u32[]{:S(2)}) %collective-permute-start.12) | collective-permute-done | bytes 196640 | tf_op jit(solution)/shard_map/ppermute | solution.py:218
  163.2 3.9 %coupled.5 = (bf16[2,64,256]{2,1,0:T(8,128)(2,1)}, bf16[2,64,256]{2,1,0:T(8,128)(2,1)}, bf16[2,64,256]{2,1,0:T(8,128)(2,1)}, bf16[2,64,256]{2,1,0:T(8,128)(2,1)}) custom-call(s32[64]{0:T(128)} %reshape.113.slot_ref, f32[64]{0:T(128)} %reshape.114.weight_ref, s32[9]{0:T(128)} %pad_add_fusion.info_ref, ...), custom_call_target="tpu_custom_call" | custom-call | flops 402653184 | bytes 1572864 | tf_op jit(solution)/shard_map/coupled/pallas_call | solution.py:161
  167.1 2.0 %collective-permute-start.17 = (bf16[2,64,256]{2,1,0:T(8,128)(2,1)}, bf16[2,64,256]{2,1,0:T(8,128)(2,1)S(1)}, u32[]{:S(2)}, u32[]{:S(2)}) collective-permute-start(bf16[2,64,256]{2,1,0:T(8,128)(2,1)} %get-tuple-element.9), channel_id=1, source_target_pairs={{0,3},{1,2},{2,1},{3,0},{4,7},{5,6},{6,5},{7,4},{8,11},{9,10},{10,... | collective-permute-start | bytes 196616 | tf_op jit(solution)/shard_map/ppermute | solution.py:218
  169.8 1.8 %collective-permute-done.17 = bf16[2,64,256]{2,1,0:T(8,128)(2,1)S(1)} collective-permute-done((bf16[2,64,256]{2,1,0:T(8,128)(2,1)}, bf16[2,64,256]{2,1,0:T(8,128)(2,1)S(1)}, u32[]{:S(2)}, u32[]{:S(2)}) %collective-permute-start.17) | collective-permute-done | bytes 65568 | tf_op jit(solution)/shard_map/ppermute | solution.py:218
  171.6 1.9 %collective-permute-done.18 = bf16[2,64,256]{2,1,0:T(8,128)(2,1)S(1)} collective-permute-done((bf16[2,64,256]{2,1,0:T(8,128)(2,1)}, bf16[2,64,256]{2,1,0:T(8,128)(2,1)S(1)}, u32[]{:S(2)}, u32[]{:S(2)}) %collective-permute-start.18) | collective-permute-done | bytes 65568 | tf_op jit(solution)/shard_map/ppermute | solution.py:218
  173.6 1.7 fusion.1
  (71 shorter events, 28.0 us)
Async XLA Ops:
  0.0 74.0 %copy-start = (f32[8,32]{1,0:T(8,128)S(1)}, f32[8,32]{1,0:T(8,128)}, u32[]{:S(2)}) copy-start(f32[8,32]{1,0:T(8,128)} %param.13) | copy-start | bytes 3076
  0.0 9.5 %collective-permute-start = (bf16[8,64,256]{2,1,0:T(8,128)(2,1)}, bf16[8,64,256]{2,1,0:T(8,128)(2,1)S(1)}, u32[]{:S(2)}, u32[]{:S(2)}) collective-permute-start(bf16[8,64,256]{2,1,0:T(8,128)(2,1)} %param.7), channel_id=1, source_target_pairs={{0,2},{1,3},{2,0},{3,1},{4,6},{5,7},{6,4},{7,5},{8,10},{9,11},{10,... | collective-permute-start | bytes 786440 | tf_op jit(solution)/shard_map/ppermute | solution.py:218
  11.6 49.4 %copy-start.2 = (bf16[8,64,256]{2,1,0:T(8,128)(2,1)S(1)}, bf16[8,64,256]{2,1,0:T(8,128)(2,1)}, u32[]{:S(2)}) copy-start(bf16[8,64,256]{2,1,0:T(8,128)(2,1)} %refs_3_.1) | copy-start | bytes 786436
  11.6 13.1 %collective-permute-start.4 = (bf16[8,128,256]{2,1,0:T(8,128)(2,1)S(1)}, bf16[8,128,256]{2,1,0:T(8,128)(2,1)S(1)}, u32[]{:S(2)}, u32[]{:S(2)}) collective-permute-start(bf16[8,128,256]{2,1,0:T(8,128)(2,1)S(1)} %get-tuple-element.19), channel_id=1, source_target_pairs={{0,8},{8,16},{16,24},{24,28},{28,20},{20,12},{12,4},{4,0},{1,9},{9... | collective-permute-start | bytes 1572872 | tf_op jit(solution)/shard_map/ppermute | solution.py:189
  13.4 12.8 %collective-permute-start.1 = (bf16[8,128,256]{2,1,0:T(8,128)(2,1)S(1)}, bf16[8,128,256]{2,1,0:T(8,128)(2,1)S(1)}, u32[]{:S(2)}, u32[]{:S(2)}) collective-permute-start(bf16[8,128,256]{2,1,0:T(8,128)(2,1)S(1)} %get-tuple-element.19), channel_id=1, source_target_pairs={{8,0},{16,8},{24,16},{28,24},{20,28},{12,20},{4,12},{0,4},{9,1},{1... | collective-permute-start | bytes 1572872 | tf_op jit(solution)/shard_map/ppermute | solution.py:190
  24.7 12.2 %collective-permute-start.5 = (bf16[8,128,256]{2,1,0:T(8,128)(2,1)S(1)}, bf16[8,128,256]{2,1,0:T(8,128)(2,1)S(1)}, u32[]{:S(2)}, u32[]{:S(2)}) collective-permute-start(bf16[8,128,256]{2,1,0:T(8,128)(2,1)S(1)} %collective-permute-done.4), channel_id=1, source_target_pairs={{0,8},{8,16},{16,24},{24,28},{28,20},{20,12},{12,4},{4,0},{1,9},{9... | collective-permute-start | bytes 1572872 | tf_op jit(solution)/shard_map/ppermute | solution.py:189
  26.3 12.1 %collective-permute-start.2 = (bf16[8,128,256]{2,1,0:T(8,128)(2,1)S(1)}, bf16[8,128,256]{2,1,0:T(8,128)(2,1)S(1)}, u32[]{:S(2)}, u32[]{:S(2)}) collective-permute-start(bf16[8,128,256]{2,1,0:T(8,128)(2,1)S(1)} %collective-permute-done.1), channel_id=1, source_target_pairs={{8,0},{16,8},{24,16},{28,24},{20,28},{12,20},{4,12},{0,4},{9,1},{1... | collective-permute-start | bytes 1572872 | tf_op jit(solution)/shard_map/ppermute | solution.py:190
  36.9 12.0 %collective-permute-start.6 = (bf16[8,128,256]{2,1,0:T(8,128)(2,1)S(1)}, bf16[8,128,256]{2,1,0:T(8,128)(2,1)S(1)}, u32[]{:S(2)}, u32[]{:S(2)}) collective-permute-start(bf16[8,128,256]{2,1,0:T(8,128)(2,1)S(1)} %collective-permute-done.5), channel_id=1, source_target_pairs={{0,8},{8,16},{16,24},{24,28},{28,20},{20,12},{12,4},{4,0},{1,9},{9... | collective-permute-start | bytes 1572872 | tf_op jit(solution)/shard_map/ppermute | solution.py:189
  38.3 12.9 %collective-permute-start.3 = (bf16[8,128,256]{2,1,0:T(8,128)(2,1)S(1)}, bf16[8,128,256]{2,1,0:T(8,128)(2,1)S(1)}, u32[]{:S(2)}, u32[]{:S(2)}) collective-permute-start(bf16[8,128,256]{2,1,0:T(8,128)(2,1)S(1)} %collective-permute-done.2), channel_id=1, source_target_pairs={{8,0},{16,8},{24,16},{28,24},{20,28},{12,20},{4,12},{0,4},{9,1},{1... | collective-permute-start | bytes 1572872 | tf_op jit(solution)/shard_map/ppermute | solution.py:190
  49.0 6.4 %collective-permute-start.7 = (bf16[4,128,256]{2,1,0:T(8,128)(2,1)S(1)}, bf16[4,128,256]{2,1,0:T(8,128)(2,1)S(1)}, u32[]{:S(2)}, u32[]{:S(2)}) collective-permute-start(bf16[4,128,256]{2,1,0:T(8,128)(2,1)S(1)} %slice.8), channel_id=1, source_target_pairs={{0,8},{8,16},{16,24},{24,28},{28,20},{20,12},{12,4},{4,0},{1,9},{9... | collective-permute-start | bytes 786440 | tf_op jit(solution)/shard_map/ppermute | solution.py:193
  51.3 6.4 %collective-permute-start.8 = (bf16[4,128,256]{2,1,0:T(8,128)(2,1)S(1)}, bf16[4,128,256]{2,1,0:T(8,128)(2,1)S(1)}, u32[]{:S(2)}, u32[]{:S(2)}) collective-permute-start(bf16[4,128,256]{2,1,0:T(8,128)(2,1)S(1)} %slice.9), channel_id=1, source_target_pairs={{8,0},{16,8},{24,16},{28,24},{20,28},{12,20},{4,12},{0,4},{9,1},{1... | collective-permute-start | bytes 786440 | tf_op jit(solution)/shard_map/ppermute | solution.py:194
  61.0 82.8 %collective-permute-start.9 = (bf16[64,128,256]{2,1,0:T(8,128)(2,1)}, bf16[64,128,256]{2,1,0:T(8,128)(2,1)}, u32[]{:S(2)}, u32[]{:S(2)}) collective-permute-start(bf16[64,128,256]{2,1,0:T(8,128)(2,1)} %constant_dynamic-update-slice_fusion.near), channel_id=1, source_target_pairs={{0,1},{1,0},{2,3},{3,2},{4,5},{5,4},{6,7},{7,6},{8,9},{9,8},{10,11... | collective-permute-start | bytes 12582920 | tf_op jit(solution)/shard_map/ppermute | solution.py:218
  64.5 77.8 %collective-permute-start.10 = (bf16[2,33,64,256]{3,2,1,0:T(8,128)(2,1)}, bf16[2,33,64,256]{3,2,1,0:T(8,128)(2,1)S(1)}, u32[]{:S(2)}, u32[]{:S(2)}) collective-permute-start(bf16[2,33,64,256]{3,2,1,0:T(8,128)(2,1)} %pad_maximum_fusion), channel_id=1, source_target_pairs={{0,1},{1,0},{2,3},{3,2},{4,5},{5,4},{6,7},{7,6},{8,9},{9,8},{10,11... | collective-permute-start | bytes 6488072 | tf_op jit(solution)/shard_map/ppermute | solution.py:218
  67.3 6.7 %copy-start.5 = (s32[8]{0:T(128)S(1)}, s32[8]{0:T(128)}, u32[]{:S(2)}) copy-start(s32[8]{0:T(128)} %param.8) | copy-start | bytes 100
  68.6 39.0 %collective-permute-start.15 = (bf16[2,25,64,256]{3,2,1,0:T(8,128)(2,1)}, bf16[2,25,64,256]{3,2,1,0:T(8,128)(2,1)}, u32[]{:S(2)}, u32[]{:S(2)}) collective-permute-start(bf16[2,25,64,256]{3,2,1,0:T(8,128)(2,1)} %pad_maximum_fusion.1), channel_id=1, source_target_pairs={{0,2},{1,3},{2,0},{3,1},{4,6},{5,7},{6,4},{7,5},{8,10},{9,11},{10,... | collective-permute-start | bytes 4915208 | tf_op jit(solution)/shard_map/ppermute | solution.py:218
  71.4 70.3 %collective-permute-start.16 = (bf16[2,25,64,256]{3,2,1,0:T(8,128)(2,1)}, bf16[2,25,64,256]{3,2,1,0:T(8,128)(2,1)}, u32[]{:S(2)}, u32[]{:S(2)}) collective-permute-start(bf16[2,25,64,256]{3,2,1,0:T(8,128)(2,1)} %pad_maximum_fusion.2), channel_id=1, source_target_pairs={{0,3},{1,2},{2,1},{3,0},{4,7},{5,6},{6,5},{7,4},{8,11},{9,10},{10,... | collective-permute-start | bytes 4915208 | tf_op jit(solution)/shard_map/ppermute | solution.py:218
  72.5 82.4 %collective-permute-start.13 = (bf16[2,5,64,256]{3,2,1,0:T(8,128)(2,1)S(1)}, bf16[2,5,64,256]{3,2,1,0:T(8,128)(2,1)S(1)}, u32[]{:S(2)}, u32[]{:S(2)}) collective-permute-start(bf16[2,5,64,256]{3,2,1,0:T(8,128)(2,1)S(1)} %get-tuple-element.16), channel_id=1, source_target_pairs={{0,2},{1,3},{2,0},{3,1},{4,6},{5,7},{6,4},{7,5},{8,10},{9,11},{10,... | collective-permute-start | bytes 983048 | tf_op jit(solution)/shard_map/ppermute | solution.py:218
  107.6 48.1 %collective-permute-start.14 = (bf16[2,5,64,256]{3,2,1,0:T(8,128)(2,1)S(1)}, bf16[2,5,64,256]{3,2,1,0:T(8,128)(2,1)S(1)}, u32[]{:S(2)}, u32[]{:S(2)}) collective-permute-start(bf16[2,5,64,256]{3,2,1,0:T(8,128)(2,1)S(1)} %get-tuple-element.15), channel_id=1, source_target_pairs={{0,3},{1,2},{2,1},{3,0},{4,7},{5,6},{6,5},{7,4},{8,11},{9,10},{10,... | collective-permute-start | bytes 983048 | tf_op jit(solution)/shard_map/ppermute | solution.py:218
  141.7 19.2 %collective-permute-start.11 = (bf16[2,3,64,256]{3,2,1,0:T(8,128)(2,1)}, bf16[2,3,64,256]{3,2,1,0:T(8,128)(2,1)}, u32[]{:S(2)}, u32[]{:S(2)}) collective-permute-start(bf16[2,3,64,256]{3,2,1,0:T(8,128)(2,1)} %get-tuple-element.18), channel_id=1, source_target_pairs={{0,2},{1,3},{2,0},{3,1},{4,6},{5,7},{6,4},{7,5},{8,10},{9,11},{10,... | collective-permute-start | bytes 589832 | tf_op jit(solution)/shard_map/ppermute | solution.py:218
  142.3 1.6 copy-start.1
  142.3 21.0 %collective-permute-start.12 = (bf16[2,3,64,256]{3,2,1,0:T(8,128)(2,1)}, bf16[2,3,64,256]{3,2,1,0:T(8,128)(2,1)}, u32[]{:S(2)}, u32[]{:S(2)}) collective-permute-start(bf16[2,3,64,256]{3,2,1,0:T(8,128)(2,1)} %get-tuple-element.17), channel_id=1, source_target_pairs={{0,3},{1,2},{2,1},{3,0},{4,7},{5,6},{6,5},{7,4},{8,11},{9,10},{10,... | collective-permute-start | bytes 589832 | tf_op jit(solution)/shard_map/ppermute | solution.py:218
  167.1 4.5 %collective-permute-start.17 = (bf16[2,64,256]{2,1,0:T(8,128)(2,1)}, bf16[2,64,256]{2,1,0:T(8,128)(2,1)S(1)}, u32[]{:S(2)}, u32[]{:S(2)}) collective-permute-start(bf16[2,64,256]{2,1,0:T(8,128)(2,1)} %get-tuple-element.9), channel_id=1, source_target_pairs={{0,3},{1,2},{2,1},{3,0},{4,7},{5,6},{6,5},{7,4},{8,11},{9,10},{10,... | collective-permute-start | bytes 196616 | tf_op jit(solution)/shard_map/ppermute | solution.py:218
  169.1 4.5 %collective-permute-start.18 = (bf16[2,64,256]{2,1,0:T(8,128)(2,1)}, bf16[2,64,256]{2,1,0:T(8,128)(2,1)S(1)}, u32[]{:S(2)}, u32[]{:S(2)}) collective-permute-start(bf16[2,64,256]{2,1,0:T(8,128)(2,1)} %get-tuple-element.10), channel_id=1, source_target_pairs={{0,2},{1,3},{2,0},{3,1},{4,6},{5,7},{6,4},{7,5},{8,10},{9,11},{10,... | collective-permute-start | bytes 196616 | tf_op jit(solution)/shard_map/ppermute | solution.py:218
  169.6 3.9 %collective-permute-start.19 = (bf16[2,64,256]{2,1,0:T(8,128)(2,1)}, bf16[2,64,256]{2,1,0:T(8,128)(2,1)S(1)}, u32[]{:S(2)}, u32[]{:S(2)}) collective-permute-start(bf16[2,64,256]{2,1,0:T(8,128)(2,1)} %get-tuple-element.11), channel_id=1, source_target_pairs={{0,1},{1,0},{2,3},{3,2},{4,5},{5,4},{6,7},{7,6},{8,9},{9,8},{10,11... | collective-permute-start | bytes 196616 | tf_op jit(solution)/shard_map/ppermute | solution.py:218
  (2 other events, 1.4 us)

commit v3 on v2

--- a/solution.py
+++ b/solution.py
@@ -8,38 +8,47 @@
 
 CHUNKS = (24, 29)
 RING_MAX = 8
+VMEM_LIMIT = 60 * 2**20
 
 
 def coupled_kernel(
-    first, last, size, start, stride, offsets,
-    slot_ref, weight_ref, info_ref, near, far, own, *refs,
+    first, last, size, after, start, stride, offsets, own_pairs,
+    slots, weights, info, near, far, own, *refs,
 ):
     refs = list(refs)
     ways = len(offsets) + 1
-    own_pairs = (info_ref.shape[0] - 1 - ways) // 2
     got = [refs.pop(0) for _ in range(ways - 1)]
     if first:
         exch, fock = refs.pop(0), refs.pop(0)
     else:
         acc = refs.pop(0)
+    ready_left = refs.pop(0) if last else None
     outs = [refs.pop(0) for _ in range(ways if last else 1)]
+    ahead = refs.pop(0) if after else None
+    slot_ref, weight_ref, info_ref, scalar_sem = (refs.pop(0) for _ in range(4))
     left, right, proj, left_sem, right_sem = (refs.pop(0) for _ in range(5))
+    ahead_sem = refs.pop(0) if after else None
     group, share, width = right.shape[1], right.shape[3], right.shape[4]
     order = list(range(0, ways, 2)) + list(range(1, ways, 2))
     rounds = size // group
-    column = info_ref[0]
+    column = lax.axis_index("cols")
+    scalars = [
+        pltpu.make_async_copy(source, target, scalar_sem.at[i])
+        for i, (source, target) in enumerate(
+            ((slots, slot_ref), (weights, weight_ref), (info, info_ref)))
+    ]
+    for copy in scalars:
+        copy.start()
 
     def block(k):
-        return info_ref[1 + 2 * own_pairs + k]
+        return column ^ k
 
     def fetch_partner(slot, place, sem):
         pltpu.make_async_copy(near.at[slot], place.at[0], sem).start()
         pltpu.make_async_copy(far.at[slot], place.at[1], sem).start()
 
-    def fetch(r, _):
+    def fetch_pieces(r, _):
         m, q = lax.div(r, rounds), lax.rem(r, rounds) * group
-        for g in range(group):
-            fetch_partner(slot_ref[m * stride + start + q + g], left.at[r, g], left_sem.at[r])
         pltpu.make_async_copy(
             own.at[column * own_pairs + m, pl.ds(start + q, group)],
             right.at[r, :, block(0)], right_sem.at[r]).start()
@@ -47,6 +56,15 @@
             pltpu.make_async_copy(
                 got[k - 1].at[m, pl.ds(offsets[k - 1] + q, group)],
                 right.at[r, :, block(k)], right_sem.at[r]).start()
+        if last:
+            pltpu.make_async_copy(
+                ready_left.at[pl.ds(r * group, group)], left.at[r], left_sem.at[r]).start()
+        return 0
+
+    def fetch_partners(r):
+        m, q = lax.div(r, rounds), lax.rem(r, rounds) * group
+        for g in range(group):
+            fetch_partner(slot_ref[m * stride + start + q + g], left.at[r, g], left_sem.at[r])
         return 0
 
     if first:
@@ -54,7 +72,6 @@
         for m in range(own_pairs):
             pltpu.make_async_copy(
                 fock.at[column * own_pairs + m], whole.at[m], whole_sem.at[m]).start()
-            fetch_partner(info_ref[1 + own_pairs + m], mine.at[m], mine_sem.at[m])
             pltpu.make_async_copy(
                 exch.at[column * own_pairs + m], base.at[m, block(0)], base_sem.at[m]).start()
             for k in range(1, ways):
@@ -65,7 +82,23 @@
         whole, whole_sem = refs
         for m in range(own_pairs):
             pltpu.make_async_copy(acc.at[m], whole.at[m], whole_sem.at[m]).start()
-    lax.fori_loop(0, own_pairs * rounds, fetch, 0)
+
+    def fetch(r, _):
+        fetch_pieces(r, 0)
+        return fetch_partners(r)
+
+    if last:
+        lax.fori_loop(0, own_pairs * rounds, fetch_pieces, 0)
+    for copy in scalars:
+        copy.wait()
+    if first:
+        for m in range(own_pairs):
+            fetch_partner(info_ref[own_pairs + m], mine.at[m], mine_sem.at[m])
+    if not last:
+        lax.fori_loop(0, own_pairs * rounds, fetch, 0)
+    for u in range(own_pairs * after):
+        fetch_partner(
+            slot_ref[u // after * stride + start + size + u % after], ahead.at[u], ahead_sem)
 
     def ready(ref, sem, i):
         pltpu.make_async_copy(ref.at[i], ref.at[i], sem.at[i]).wait()
@@ -110,7 +143,7 @@
 
         lax.fori_loop(0, rounds, body, 0)
         if last:
-            count = info_ref[1 + m]
+            count = info_ref[m]
             row = lax.broadcasted_iota(jnp.int32, (width, width), 0)
             col = lax.broadcasted_iota(jnp.int32, (width, width), 1)
             keep = (row < count) & (col < count)
@@ -118,10 +151,12 @@
             for k in range(ways):
                 rows = pl.ds(pl.multiple_of(block(k) * share, share), share)
                 outs[k][m] = total[m, rows, :].astype(jnp.bfloat16)
+    if after:
+        pltpu.make_async_copy(ahead, ahead, ahead_sem).wait()
 
 
 def run_chunk(
-    start, size, first, last, near, far, own_pieces, got, slots, weights, info, acc, exch, fock
+    start, size, after, first, last, ready_left, near, far, own_pieces, got, slots, weights, info, acc, exch, fock
 ):
     own_pairs = got[0][0].shape[0]
     ways = len(got) + 1
@@ -129,24 +164,35 @@
     share = own_pieces.shape[2]
     units = own_pairs * size
     anywhere = pl.BlockSpec(memory_space=pl.ANY)
-    operands = [near, far, own_pieces] + [piece for piece, _ in got]
+    operands = [slots, weights, info, near, far, own_pieces] + [piece for piece, _ in got]
     operands += [exch, fock] if first else [acc]
+    if last:
+        operands.append(ready_left)
     inside = pl.BlockSpec(memory_space=pltpu.VMEM)
     if last:
         out_shape = [jax.ShapeDtypeStruct((own_pairs, share, width), jnp.bfloat16)] * ways
         out_specs = [inside] * ways
     else:
-        out_shape = jax.ShapeDtypeStruct((own_pairs, width, width), jnp.float32)
-        out_specs = inside
+        out_shape = [jax.ShapeDtypeStruct((own_pairs, width, width), jnp.float32)]
+        out_specs = [inside]
+    if after:
+        out_shape.append(jax.ShapeDtypeStruct((own_pairs * after, 2, width // 2, width), jnp.bfloat16))
+        out_specs.append(inside)
     group = max(g for g in (1, 2, 3, 4, 5) if size % g == 0)
     rounds = units // group
     scratch = [
+        pltpu.SMEM(slots.shape, slots.dtype),
+        pltpu.SMEM(weights.shape, weights.dtype),
+        pltpu.SMEM(info.shape, info.dtype),
+        pltpu.SemaphoreType.DMA((3,)),
         pltpu.VMEM((rounds, group, 2, width // 2, width), jnp.bfloat16),
         pltpu.VMEM((rounds, group, ways, share, width), jnp.bfloat16),
         pltpu.VMEM((group, ways, share, width), jnp.bfloat16),
         pltpu.SemaphoreType.DMA((rounds,)),
         pltpu.SemaphoreType.DMA((rounds,)),
     ]
+    if after:
+        scratch.append(pltpu.SemaphoreType.DMA)
     pair_sems = pltpu.SemaphoreType.DMA((own_pairs,))
     if first:
         scratch += [
@@ -160,19 +206,17 @@
     stride = slots.shape[0] // own_pairs
     return pl.pallas_call(
         functools.partial(
-            coupled_kernel, first, last, size, start, stride, tuple(o for _, o in got)),
+            coupled_kernel, first, last, size, after, start, stride,
+            tuple(o for _, o in got), own_pairs),
         out_shape=out_shape,
-        grid_spec=pltpu.PrefetchScalarGridSpec(
-            num_scalar_prefetch=3,
-            grid=(),
-            in_specs=[anywhere] * len(operands),
-            out_specs=out_specs,
-            scratch_shapes=scratch,
-        ),
+        in_specs=[anywhere] * len(operands),
+        out_specs=out_specs,
+        scratch_shapes=scratch,
         cost_estimate=pl.CostEstimate(
             flops=units * 4 * width**3, bytes_accessed=units * 4 * width**2, transcendentals=0),
+        compiler_params=pltpu.CompilerParams(vmem_limit_bytes=VMEM_LIMIT),
         name="coupled",
-    )(slots, weights, info, *operands)
+    )(*operands)
 
 
 def gather_pairs(half, count):
@@ -254,13 +298,17 @@
     own_counts = lax.dynamic_slice_in_dim(pno_counts, begin, own_pairs, 0)
     own_slots = place(lax.axis_index("pairs")) * local_pairs + begin + jnp.arange(own_pairs, dtype=jnp.int32)
     blocks = column ^ jnp.arange(ways, dtype=jnp.int32)
-    info = jnp.concatenate([column[None].astype(jnp.int32), own_counts, own_slots, blocks])
-
-    acc = None
+    info = jnp.concatenate([own_counts, own_slots])
+
+    acc = ready_left = None
     for n, (start, stop) in enumerate(bounds):
-        acc = run_chunk(
-            start, stop - start, n == 0, n == len(bounds) - 1, near, far, intersections,
+        first, last = n == 0, n == len(bounds) - 1
+        after = bounds[n + 1][1] - stop if n == len(bounds) - 2 else 0
+        outs = run_chunk(
+            start, stop - start, after, first, last, ready_left, near, far, intersections,
             got[n], slots.reshape(-1), weights.reshape(-1), info, acc, exchange_blocks, fock_blocks)
+        acc = outs if last else outs[0]
+        ready_left = outs[1] if after else None
     arrived = [acc[0]] + [swap(acc[k], k) for k in range(1, ways)]
     spots = blocks[:, None, None, None]
     shared = arrived[0][None]

time: 176 us -> 176 us (level)
    unnamed x19 -> x23, local copies, waits for them, and re-layouts: 6.46 us -> 7.23 us
  transfers between devices with their start and end apart: 20 -> 20, of which waited for: 13 -> 12; matrix products, arithmetic and copies ran while one was open for 11% -> 11% of each run, Pallas kernels for 9% -> 9%
where the time goes in v3:
time: 176 us; the launch traced here: 175 us
  waiting for transfers between devices  109 us (62%)
  starting transfers between devices  19.2 us (11%)
  Pallas kernels  19.2 us (11%)
  local copies, waits for them, and re-layouts  17 us (10%)
  other arithmetic  10.8 us (6%)
    ppermute x12, waiting for transfers between devices, swap(): return lax.ppermute(array, 'cols', [(c, c ^ k) for c in range(ways)])  74.3 us
    ppermute x3, waiting for transfers between devices, gather_pairs(): forward = lax.ppermute(forward, 'pairs', ahead)  31.2 us
    pallas_call x3, Pallas kernels, run_chunk(): pl.pallas_call(functools.partial(coupled_kernel, first, last, size, after...  19.2 us
    ppermute x12, starting transfers between devices, swap(): return lax.ppermute(array, 'cols', [(c, c ^ k) for c in range(ways)])  11 us
    unnamed x23, local copies, waits for them, and re-layouts  7.23 us
    dynamic_slice x4, local copies, waits for them, and re-layouts, moved(): lax.dynamic_slice(intersections, (begin, start, 0, 0), (own_pairs, stop -...  7.01 us
    ppermute x3, starting transfers between devices, gather_pairs(): forward = lax.ppermute(forward, 'pairs', ahead)  4.78 us
    concatenate x3, other arithmetic, moved(): piece = jnp.concatenate([piece, extra[:, None]], axis=1)  4.22 us
  transfers between devices with their start and end apart: 20, of which 12 were waited for; matrix products, arithmetic and copies ran while one was open for 11% of the time, Pallas kernels for 9%

profile of v3, /device:TPU:0, one launch (start us, length us, event | category | flops | bytes accessed | tf_op | source)
XLA Modules:
  0.0 175.2 jit_solution(13484411807462793253)
XLA Ops:
  0.0 3.0 %collective-permute-start = (bf16[8,64,256]{2,1,0:T(8,128)(2,1)}, bf16[8,64,256]{2,1,0:T(8,128)(2,1)S(1)}, u32[]{:S(2)}, u32[]{:S(2)}) collective-permute-start(bf16[8,64,256]{2,1,0:T(8,128)(2,1)} %param.7), channel_id=1, source_target_pairs={{0,2},{1,3},{2,0},{3,1},{4,6},{5,7},{6,4},{7,5},{8,10},{9,11},{10,... | collective-permute-start | bytes 786440 | tf_op jit(solution)/shard_map/ppermute | solution.py:262
  4.4 5.1 %collective-permute-done = bf16[8,64,256]{2,1,0:T(8,128)(2,1)S(1)} collective-permute-done((bf16[8,64,256]{2,1,0:T(8,128)(2,1)}, bf16[8,64,256]{2,1,0:T(8,128)(2,1)S(1)}, u32[]{:S(2)}, u32[]{:S(2)}) %collective-permute-start) | collective-permute-done | bytes 262176 | tf_op jit(solution)/shard_map/ppermute | solution.py:262
  11.6 1.8 %collective-permute-start.4 = (bf16[8,128,256]{2,1,0:T(8,128)(2,1)S(1)}, bf16[8,128,256]{2,1,0:T(8,128)(2,1)S(1)}, u32[]{:S(2)}, u32[]{:S(2)}) collective-permute-start(bf16[8,128,256]{2,1,0:T(8,128)(2,1)S(1)} %get-tuple-element.23), channel_id=1, source_target_pairs={{0,8},{8,16},{16,24},{24,28},{28,20},{20,12},{12,4},{4,0},{1,9},{9... | collective-permute-start | bytes 1572872 | tf_op jit(solution)/shard_map/ppermute | solution.py:233
  13.6 11.1 %collective-permute-done.4 = bf16[8,128,256]{2,1,0:T(8,128)(2,1)S(1)} collective-permute-done((bf16[8,128,256]{2,1,0:T(8,128)(2,1)S(1)}, bf16[8,128,256]{2,1,0:T(8,128)(2,1)S(1)}, u32[]{:S(2)}, u32[]{:S(2)}) %collective-permute-start.4) | collective-permute-done | bytes 524320 | tf_op jit(solution)/shard_map/ppermute | solution.py:233
  24.7 1.5 collective-permute-start.5
  26.7 10.2 %collective-permute-done.5 = bf16[8,128,256]{2,1,0:T(8,128)(2,1)S(1)} collective-permute-done((bf16[8,128,256]{2,1,0:T(8,128)(2,1)S(1)}, bf16[8,128,256]{2,1,0:T(8,128)(2,1)S(1)}, u32[]{:S(2)}, u32[]{:S(2)}) %collective-permute-start.5) | collective-permute-done | bytes 524320 | tf_op jit(solution)/shard_map/ppermute | solution.py:233
  39.0 10.0 %collective-permute-done.6 = bf16[8,128,256]{2,1,0:T(8,128)(2,1)S(1)} collective-permute-done((bf16[8,128,256]{2,1,0:T(8,128)(2,1)S(1)}, bf16[8,128,256]{2,1,0:T(8,128)(2,1)S(1)}, u32[]{:S(2)}, u32[]{:S(2)}) %collective-permute-start.6) | collective-permute-done | bytes 524320 | tf_op jit(solution)/shard_map/ppermute | solution.py:233
  53.6 1.7 collective-permute-done.7
  56.1 1.6 collective-permute-done.8
  61.0 1.8 %constant_dynamic-slice_fusion.6 = bf16[2,32,64,256]{3,2,1,0:T(8,128)(2,1)S(1)} fusion(bf16[8,32,64,256]{3,2,1,0:T(8,128)(2,1)} %own.5, s32[]{:T(128)S(6)} %select_n.107), kind=kLoop, calls=%fused_computation.28 | loop fusion | bytes 4194308 | tf_op jit(solution)/shard_map/dynamic_slice | solution.py:278
  62.9 1.6 pad_maximum_fusion
  65.0 2.3 %constant_dynamic-slice_fusion = (bf16[2,24,64,256]{3,2,1,0:T(8,128)(2,1)S(1)}, bf16[2,24,64,256]{3,2,1,0:T(8,128)(2,1)S(1)}) fusion(bf16[8,32,64,256]{3,2,1,0:T(8,128)(2,1)} %own.5, s32[]{:T(128)S(6)} %select_n.109, s32[]{:T(128)S(6)} %select_n.108), kind=kLoop, calls=%fused_computation.22 | loop fusion | bytes 6291464 | tf_op jit(solution)/shard_map/dynamic_slice | solution.py:278
  74.7 1.8 %constant_dynamic-slice_fusion.4 = (bf16[2,3,64,256]{3,2,1,0:T(8,128)(2,1)}, bf16[2,3,64,256]{3,2,1,0:T(8,128)(2,1)}) fusion(bf16[8,32,64,256]{3,2,1,0:T(8,128)(2,1)} %own.5, s32[]{:T(128)S(6)} %select_n.109, s32[]{:T(128)S(6)} %select_n.108), kind=kLoop, calls=%fused_computation.26 | loop fusion | bytes 786440 | tf_op jit(solution)/shard_map/dynamic_slice | solution.py:278
  76.5 31.0 %collective-permute-done.15.refs_1_ = bf16[2,25,64,256]{3,2,1,0:T(8,128)(2,1)} collective-permute-done((bf16[2,25,64,256]{3,2,1,0:T(8,128)(2,1)}, bf16[2,25,64,256]{3,2,1,0:T(8,128)(2,1)}, u32[]{:S(2)}, u32[]{:S(2)}) %collective-permute-start.15) | collective-permute-done | bytes 1638432 | tf_op jit(solution)/shard_map/ppermute | solution.py:262
  109.7 32.0 %collective-permute-done.16.refs_2_ = bf16[2,25,64,256]{3,2,1,0:T(8,128)(2,1)} collective-permute-done((bf16[2,25,64,256]{3,2,1,0:T(8,128)(2,1)}, bf16[2,25,64,256]{3,2,1,0:T(8,128)(2,1)}, u32[]{:S(2)}, u32[]{:S(2)}) %collective-permute-start.16) | collective-permute-done | bytes 1638432 | tf_op jit(solution)/shard_map/ppermute | solution.py:262
  142.2 1.6 collective-permute-start.12
  143.9 11.1 %coupled.3.refs_3_ = f32[2,256,256]{2,1,0:T(8,128)} custom-call(s32[64]{0:T(128)} %reshape.113.slots, f32[64]{0:T(128)} %reshape.114.weights, s32[4]{0:T(128)} %pad_add_fusion.info, bf16[64,128,256]{2,1,0:T(8,128)(2,1)} %constant_dynamic-update-slice_fusion.near, bf16[64,128,256]{2,1,0:T(8,128)(2,1)} %collective-permute-done.9.far, ...), custom_call_target="tpu_custom_call" | custom-call | flops 3221225472 | bytes 12582912 | tf_op jit(solution)/shard_map/coupled/pallas_call | solution.py:207
  156.5 4.8 %coupled.4 = (f32[2,256,256]{2,1,0:T(8,128)}, bf16[6,2,128,256]{3,2,1,0:T(8,128)(2,1)}) custom-call(s32[64]{0:T(128)} %reshape.113.slots, f32[64]{0:T(128)} %reshape.114.weights, s32[4]{0:T(128)} %pad_add_fusion.info, bf16[64,128,256]{2,1,0:T(8,128)(2,1)} %constant_dynamic-update-slice_fusion.near, bf16[64,128,256]{2,1,0:T(8,128)(2,1)} %collective-permute-done.9.far, ...), custom_call_target="tpu_custom_call" | custom-call | flops 671088640 | bytes 2621440 | tf_op jit(solution)/shard_map/coupled/pallas_call | solution.py:207
  161.3 1.9 %collective-permute-done.12.refs_2_ = bf16[2,3,64,256]{3,2,1,0:T(8,128)(2,1)S(1)} collective-permute-done((bf16[2,3,64,256]{3,2,1,0:T(8,128)(2,1)}, bf16[2,3,64,256]{3,2,1,0:T(8,128)(2,1)S(1)}, u32[]{:S(2)}, u32[]{:S(2)}) %collective-permute-start.12) | collective-permute-done | bytes 196640 | tf_op jit(solution)/shard_map/ppermute | solution.py:262
  163.9 3.3 %coupled.5 = (bf16[2,64,256]{2,1,0:T(8,128)(2,1)}, bf16[2,64,256]{2,1,0:T(8,128)(2,1)}, bf16[2,64,256]{2,1,0:T(8,128)(2,1)}, bf16[2,64,256]{2,1,0:T(8,128)(2,1)}) custom-call(s32[64]{0:T(128)} %reshape.113.slots, f32[64]{0:T(128)} %reshape.114.weights, s32[4]{0:T(128)} %pad_add_fusion.info, bf16[64,128,256]{2,1,0:T(8,128)(2,1)} %constant_dynamic-update-slice_fusion.near, ...), custom_call_target="tpu_custom_call" | custom-call | flops 402653184 | bytes 1572864 | tf_op jit(solution)/shard_map/coupled/pallas_call | solution.py:207
  167.2 1.9 %collective-permute-start.17 = (bf16[2,64,256]{2,1,0:T(8,128)(2,1)}, bf16[2,64,256]{2,1,0:T(8,128)(2,1)S(1)}, u32[]{:S(2)}, u32[]{:S(2)}) collective-permute-start(bf16[2,64,256]{2,1,0:T(8,128)(2,1)} %get-tuple-element.13), channel_id=1, source_target_pairs={{0,3},{1,2},{2,1},{3,0},{4,7},{5,6},{6,5},{7,4},{8,11},{9,10},{10,... | collective-permute-start | bytes 196616 | tf_op jit(solution)/shard_map/ppermute | solution.py:262
  169.8 1.8 %collective-permute-done.17 = bf16[2,64,256]{2,1,0:T(8,128)(2,1)S(1)} collective-permute-done((bf16[2,64,256]{2,1,0:T(8,128)(2,1)}, bf16[2,64,256]{2,1,0:T(8,128)(2,1)S(1)}, u32[]{:S(2)}, u32[]{:S(2)}) %collective-permute-start.17) | collective-permute-done | bytes 65568 | tf_op jit(solution)/shard_map/ppermute | solution.py:262
  171.6 1.9 %collective-permute-done.18 = bf16[2,64,256]{2,1,0:T(8,128)(2,1)S(1)} collective-permute-done((bf16[2,64,256]{2,1,0:T(8,128)(2,1)}, bf16[2,64,256]{2,1,0:T(8,128)(2,1)S(1)}, u32[]{:S(2)}, u32[]{:S(2)}) %collective-permute-start.18) | collective-permute-done | bytes 65568 | tf_op jit(solution)/shard_map/ppermute | solution.py:262
  173.6 1.7 fusion.1
  (74 shorter events, 28.5 us)
Async XLA Ops:
  0.0 74.0 %copy-start = (f32[8,32]{1,0:T(8,128)S(1)}, f32[8,32]{1,0:T(8,128)}, u32[]{:S(2)}) copy-start(f32[8,32]{1,0:T(8,128)} %param.13) | copy-start | bytes 3076
  0.0 9.5 %collective-permute-start = (bf16[8,64,256]{2,1,0:T(8,128)(2,1)}, bf16[8,64,256]{2,1,0:T(8,128)(2,1)S(1)}, u32[]{:S(2)}, u32[]{:S(2)}) collective-permute-start(bf16[8,64,256]{2,1,0:T(8,128)(2,1)} %param.7), channel_id=1, source_target_pairs={{0,2},{1,3},{2,0},{3,1},{4,6},{5,7},{6,4},{7,5},{8,10},{9,11},{10,... | collective-permute-start | bytes 786440 | tf_op jit(solution)/shard_map/ppermute | solution.py:262
  11.6 49.4 %copy-start.2 = (bf16[8,64,256]{2,1,0:T(8,128)(2,1)S(1)}, bf16[8,64,256]{2,1,0:T(8,128)(2,1)}, u32[]{:S(2)}) copy-start(bf16[8,64,256]{2,1,0:T(8,128)(2,1)} %refs_3_.1) | copy-start | bytes 786436
  11.6 13.1 %collective-permute-start.4 = (bf16[8,128,256]{2,1,0:T(8,128)(2,1)S(1)}, bf16[8,128,256]{2,1,0:T(8,128)(2,1)S(1)}, u32[]{:S(2)}, u32[]{:S(2)}) collective-permute-start(bf16[8,128,256]{2,1,0:T(8,128)(2,1)S(1)} %get-tuple-element.23), channel_id=1, source_target_pairs={{0,8},{8,16},{16,24},{24,28},{28,20},{20,12},{12,4},{4,0},{1,9},{9... | collective-permute-start | bytes 1572872 | tf_op jit(solution)/shard_map/ppermute | solution.py:233
  13.4 12.8 %collective-permute-start.1 = (bf16[8,128,256]{2,1,0:T(8,128)(2,1)S(1)}, bf16[8,128,256]{2,1,0:T(8,128)(2,1)S(1)}, u32[]{:S(2)}, u32[]{:S(2)}) collective-permute-start(bf16[8,128,256]{2,1,0:T(8,128)(2,1)S(1)} %get-tuple-element.23), channel_id=1, source_target_pairs={{8,0},{16,8},{24,16},{28,24},{20,28},{12,20},{4,12},{0,4},{9,1},{1... | collective-permute-start | bytes 1572872 | tf_op jit(solution)/shard_map/ppermute | solution.py:234
  24.7 12.2 %collective-permute-start.5 = (bf16[8,128,256]{2,1,0:T(8,128)(2,1)S(1)}, bf16[8,128,256]{2,1,0:T(8,128)(2,1)S(1)}, u32[]{:S(2)}, u32[]{:S(2)}) collective-permute-start(bf16[8,128,256]{2,1,0:T(8,128)(2,1)S(1)} %collective-permute-done.4), channel_id=1, source_target_pairs={{0,8},{8,16},{16,24},{24,28},{28,20},{20,12},{12,4},{4,0},{1,9},{9... | collective-permute-start | bytes 1572872 | tf_op jit(solution)/shard_map/ppermute | solution.py:233
  26.2 12.1 %collective-permute-start.2 = (bf16[8,128,256]{2,1,0:T(8,128)(2,1)S(1)}, bf16[8,128,256]{2,1,0:T(8,128)(2,1)S(1)}, u32[]{:S(2)}, u32[]{:S(2)}) collective-permute-start(bf16[8,128,256]{2,1,0:T(8,128)(2,1)S(1)} %collective-permute-done.1), channel_id=1, source_target_pairs={{8,0},{16,8},{24,16},{28,24},{20,28},{12,20},{4,12},{0,4},{9,1},{1... | collective-permute-start | bytes 1572872 | tf_op jit(solution)/shard_map/ppermute | solution.py:234
  36.9 12.0 %collective-permute-start.6 = (bf16[8,128,256]{2,1,0:T(8,128)(2,1)S(1)}, bf16[8,128,256]{2,1,0:T(8,128)(2,1)S(1)}, u32[]{:S(2)}, u32[]{:S(2)}) collective-permute-start(bf16[8,128,256]{2,1,0:T(8,128)(2,1)S(1)} %collective-permute-done.5), channel_id=1, source_target_pairs={{0,8},{8,16},{16,24},{24,28},{28,20},{20,12},{12,4},{4,0},{1,9},{9... | collective-permute-start | bytes 1572872 | tf_op jit(solution)/shard_map/ppermute | solution.py:233
  38.3 12.9 %collective-permute-start.3 = (bf16[8,128,256]{2,1,0:T(8,128)(2,1)S(1)}, bf16[8,128,256]{2,1,0:T(8,128)(2,1)S(1)}, u32[]{:S(2)}, u32[]{:S(2)}) collective-permute-start(bf16[8,128,256]{2,1,0:T(8,128)(2,1)S(1)} %collective-permute-done.2), channel_id=1, source_target_pairs={{8,0},{16,8},{24,16},{28,24},{20,28},{12,20},{4,12},{0,4},{9,1},{1... | collective-permute-start | bytes 1572872 | tf_op jit(solution)/shard_map/ppermute | solution.py:234
  49.0 6.4 %collective-permute-start.7 = (bf16[4,128,256]{2,1,0:T(8,128)(2,1)S(1)}, bf16[4,128,256]{2,1,0:T(8,128)(2,1)S(1)}, u32[]{:S(2)}, u32[]{:S(2)}) collective-permute-start(bf16[4,128,256]{2,1,0:T(8,128)(2,1)S(1)} %slice.8), channel_id=1, source_target_pairs={{0,8},{8,16},{16,24},{24,28},{28,20},{20,12},{12,4},{4,0},{1,9},{9... | collective-permute-start | bytes 786440 | tf_op jit(solution)/shard_map/ppermute | solution.py:237
  51.3 6.4 %collective-permute-start.8 = (bf16[4,128,256]{2,1,0:T(8,128)(2,1)S(1)}, bf16[4,128,256]{2,1,0:T(8,128)(2,1)S(1)}, u32[]{:S(2)}, u32[]{:S(2)}) collective-permute-start(bf16[4,128,256]{2,1,0:T(8,128)(2,1)S(1)} %slice.9), channel_id=1, source_target_pairs={{8,0},{16,8},{24,16},{28,24},{20,28},{12,20},{4,12},{0,4},{9,1},{1... | collective-permute-start | bytes 786440 | tf_op jit(solution)/shard_map/ppermute | solution.py:238
  61.0 82.8 %collective-permute-start.9 = (bf16[64,128,256]{2,1,0:T(8,128)(2,1)}, bf16[64,128,256]{2,1,0:T(8,128)(2,1)}, u32[]{:S(2)}, u32[]{:S(2)}) collective-permute-start(bf16[64,128,256]{2,1,0:T(8,128)(2,1)} %constant_dynamic-update-slice_fusion.near), channel_id=1, source_target_pairs={{0,1},{1,0},{2,3},{3,2},{4,5},{5,4},{6,7},{7,6},{8,9},{9,8},{10,11... | collective-permute-start | bytes 12582920 | tf_op jit(solution)/shard_map/ppermute | solution.py:262
  64.5 77.8 %collective-permute-start.10 = (bf16[2,33,64,256]{3,2,1,0:T(8,128)(2,1)}, bf16[2,33,64,256]{3,2,1,0:T(8,128)(2,1)S(1)}, u32[]{:S(2)}, u32[]{:S(2)}) collective-permute-start(bf16[2,33,64,256]{3,2,1,0:T(8,128)(2,1)} %pad_maximum_fusion), channel_id=1, source_target_pairs={{0,1},{1,0},{2,3},{3,2},{4,5},{5,4},{6,7},{7,6},{8,9},{9,8},{10,11... | collective-permute-start | bytes 6488072 | tf_op jit(solution)/shard_map/ppermute | solution.py:262
  67.3 6.7 %copy-start.7 = (s32[8]{0:T(128)S(1)}, s32[8]{0:T(128)}, u32[]{:S(2)}) copy-start(s32[8]{0:T(128)} %param.8) | copy-start | bytes 100
  68.6 39.0 %collective-permute-start.15 = (bf16[2,25,64,256]{3,2,1,0:T(8,128)(2,1)}, bf16[2,25,64,256]{3,2,1,0:T(8,128)(2,1)}, u32[]{:S(2)}, u32[]{:S(2)}) collective-permute-start(bf16[2,25,64,256]{3,2,1,0:T(8,128)(2,1)} %pad_maximum_fusion.1), channel_id=1, source_target_pairs={{0,2},{1,3},{2,0},{3,1},{4,6},{5,7},{6,4},{7,5},{8,10},{9,11},{10,... | collective-permute-start | bytes 4915208 | tf_op jit(solution)/shard_map/ppermute | solution.py:262
  71.4 70.3 %collective-permute-start.16 = (bf16[2,25,64,256]{3,2,1,0:T(8,128)(2,1)}, bf16[2,25,64,256]{3,2,1,0:T(8,128)(2,1)}, u32[]{:S(2)}, u32[]{:S(2)}) collective-permute-start(bf16[2,25,64,256]{3,2,1,0:T(8,128)(2,1)} %pad_maximum_fusion.2), channel_id=1, source_target_pairs={{0,3},{1,2},{2,1},{3,0},{4,7},{5,6},{6,5},{7,4},{8,11},{9,10},{10,... | collective-permute-start | bytes 4915208 | tf_op jit(solution)/shard_map/ppermute | solution.py:262
  72.5 82.5 %collective-permute-start.13 = (bf16[2,5,64,256]{3,2,1,0:T(8,128)(2,1)S(1)}, bf16[2,5,64,256]{3,2,1,0:T(8,128)(2,1)S(1)}, u32[]{:S(2)}, u32[]{:S(2)}) collective-permute-start(bf16[2,5,64,256]{3,2,1,0:T(8,128)(2,1)S(1)} %get-tuple-element.20), channel_id=1, source_target_pairs={{0,2},{1,3},{2,0},{3,1},{4,6},{5,7},{6,4},{7,5},{8,10},{9,11},{10,... | collective-permute-start | bytes 983048 | tf_op jit(solution)/shard_map/ppermute | solution.py:262
  107.6 48.1 %collective-permute-start.14 = (bf16[2,5,64,256]{3,2,1,0:T(8,128)(2,1)S(1)}, bf16[2,5,64,256]{3,2,1,0:T(8,128)(2,1)S(1)}, u32[]{:S(2)}, u32[]{:S(2)}) collective-permute-start(bf16[2,5,64,256]{3,2,1,0:T(8,128)(2,1)S(1)} %get-tuple-element.19), channel_id=1, source_target_pairs={{0,3},{1,2},{2,1},{3,0},{4,7},{5,6},{6,5},{7,4},{8,11},{9,10},{10,... | collective-permute-start | bytes 983048 | tf_op jit(solution)/shard_map/ppermute | solution.py:262
  141.7 19.6 %collective-permute-start.11 = (bf16[2,3,64,256]{3,2,1,0:T(8,128)(2,1)}, bf16[2,3,64,256]{3,2,1,0:T(8,128)(2,1)S(1)}, u32[]{:S(2)}, u32[]{:S(2)}) collective-permute-start(bf16[2,3,64,256]{3,2,1,0:T(8,128)(2,1)} %get-tuple-element.22), channel_id=1, source_target_pairs={{0,2},{1,3},{2,0},{3,1},{4,6},{5,7},{6,4},{7,5},{8,10},{9,11},{10,... | collective-permute-start | bytes 589832 | tf_op jit(solution)/shard_map/ppermute | solution.py:262
  142.2 21.0 %collective-permute-start.12 = (bf16[2,3,64,256]{3,2,1,0:T(8,128)(2,1)}, bf16[2,3,64,256]{3,2,1,0:T(8,128)(2,1)S(1)}, u32[]{:S(2)}, u32[]{:S(2)}) collective-permute-start(bf16[2,3,64,256]{3,2,1,0:T(8,128)(2,1)} %get-tuple-element.21), channel_id=1, source_target_pairs={{0,3},{1,2},{2,1},{3,0},{4,7},{5,6},{6,5},{7,4},{8,11},{9,10},{10,... | collective-permute-start | bytes 589832 | tf_op jit(solution)/shard_map/ppermute | solution.py:262
  161.3 1.9 %copy-start.5 = (bf16[2,3,64,256]{3,2,1,0:T(8,128)(2,1)}, bf16[2,3,64,256]{3,2,1,0:T(8,128)(2,1)S(1)}, u32[]{:S(2)}) copy-start(bf16[2,3,64,256]{3,2,1,0:T(8,128)(2,1)S(1)} %collective-permute-done.11.refs_1_) | copy-start | bytes 589828
  167.2 4.4 %collective-permute-start.17 = (bf16[2,64,256]{2,1,0:T(8,128)(2,1)}, bf16[2,64,256]{2,1,0:T(8,128)(2,1)S(1)}, u32[]{:S(2)}, u32[]{:S(2)}) collective-permute-start(bf16[2,64,256]{2,1,0:T(8,128)(2,1)} %get-tuple-element.13), channel_id=1, source_target_pairs={{0,3},{1,2},{2,1},{3,0},{4,7},{5,6},{6,5},{7,4},{8,11},{9,10},{10,... | collective-permute-start | bytes 196616 | tf_op jit(solution)/shard_map/ppermute | solution.py:262
  169.1 4.5 %collective-permute-start.18 = (bf16[2,64,256]{2,1,0:T(8,128)(2,1)}, bf16[2,64,256]{2,1,0:T(8,128)(2,1)S(1)}, u32[]{:S(2)}, u32[]{:S(2)}) collective-permute-start(bf16[2,64,256]{2,1,0:T(8,128)(2,1)} %get-tuple-element.14), channel_id=1, source_target_pairs={{0,2},{1,3},{2,0},{3,1},{4,6},{5,7},{6,4},{7,5},{8,10},{9,11},{10,... | collective-permute-start | bytes 196616 | tf_op jit(solution)/shard_map/ppermute | solution.py:262
  169.6 4.0 %collective-permute-start.19 = (bf16[2,64,256]{2,1,0:T(8,128)(2,1)}, bf16[2,64,256]{2,1,0:T(8,128)(2,1)S(1)}, u32[]{:S(2)}, u32[]{:S(2)}) collective-permute-start(bf16[2,64,256]{2,1,0:T(8,128)(2,1)} %get-tuple-element.15), channel_id=1, source_target_pairs={{0,1},{1,0},{2,3},{3,2},{4,5},{5,4},{6,7},{7,6},{8,9},{9,8},{10,11... | collective-permute-start | bytes 196616 | tf_op jit(solution)/shard_map/ppermute | solution.py:262
  (4 other events, 3.8 us)

commit v4 on v3

--- a/solution.py
+++ b/solution.py
@@ -6,13 +6,13 @@
 from jax.experimental.pallas import tpu as pltpu
 from jax.sharding import PartitionSpec as P
 
-CHUNKS = (24, 29)
+CHUNKS = (20, 28)
 RING_MAX = 8
 VMEM_LIMIT = 60 * 2**20
 
 
 def coupled_kernel(
-    first, last, size, after, start, stride, offsets, own_pairs,
+    taken, first, last, size, after, start, stride, offsets, own_pairs, base_pair, pairs_here,
     slots, weights, info, near, far, own, *refs,
 ):
     refs = list(refs)
@@ -22,7 +22,7 @@
         exch, fock = refs.pop(0), refs.pop(0)
     else:
         acc = refs.pop(0)
-    ready_left = refs.pop(0) if last else None
+    ready_left = refs.pop(0) if taken else None
     outs = [refs.pop(0) for _ in range(ways if last else 1)]
     ahead = refs.pop(0) if after else None
     slot_ref, weight_ref, info_ref, scalar_sem = (refs.pop(0) for _ in range(4))
@@ -50,13 +50,13 @@
     def fetch_pieces(r, _):
         m, q = lax.div(r, rounds), lax.rem(r, rounds) * group
         pltpu.make_async_copy(
-            own.at[column * own_pairs + m, pl.ds(start + q, group)],
+            own.at[column * own_pairs + base_pair + m, pl.ds(start + q, group)],
             right.at[r, :, block(0)], right_sem.at[r]).start()
         for k in range(1, ways):
             pltpu.make_async_copy(
-                got[k - 1].at[m, pl.ds(offsets[k - 1] + q, group)],
+                got[k - 1].at[offsets[k - 1][0] + m, pl.ds(offsets[k - 1][1] + q, group)],
                 right.at[r, :, block(k)], right_sem.at[r]).start()
-        if last:
+        if taken:
             pltpu.make_async_copy(
                 ready_left.at[pl.ds(r * group, group)], left.at[r], left_sem.at[r]).start()
         return 0
@@ -64,7 +64,7 @@
     def fetch_partners(r):
         m, q = lax.div(r, rounds), lax.rem(r, rounds) * group
         for g in range(group):
-            fetch_partner(slot_ref[m * stride + start + q + g], left.at[r, g], left_sem.at[r])
+            fetch_partner(slot_ref[(base_pair + m) * stride + start + q + g], left.at[r, g], left_sem.at[r])
         return 0
 
     if first:
@@ -80,25 +80,25 @@
                 ).start()
     else:
         whole, whole_sem = refs
-        for m in range(own_pairs):
-            pltpu.make_async_copy(acc.at[m], whole.at[m], whole_sem.at[m]).start()
+        for m in range(pairs_here):
+            pltpu.make_async_copy(acc.at[base_pair + m], whole.at[m], whole_sem.at[m]).start()
 
     def fetch(r, _):
         fetch_pieces(r, 0)
         return fetch_partners(r)
 
-    if last:
-        lax.fori_loop(0, own_pairs * rounds, fetch_pieces, 0)
+    if taken:
+        lax.fori_loop(0, pairs_here * rounds, fetch_pieces, 0)
     for copy in scalars:
         copy.wait()
     if first:
         for m in range(own_pairs):
             fetch_partner(info_ref[own_pairs + m], mine.at[m], mine_sem.at[m])
-    if not last:
-        lax.fori_loop(0, own_pairs * rounds, fetch, 0)
-    for u in range(own_pairs * after):
+    if not taken:
+        lax.fori_loop(0, pairs_here * rounds, fetch, 0)
+    for u in range(after):
         fetch_partner(
-            slot_ref[u // after * stride + start + size + u % after], ahead.at[u], ahead_sem)
+            slot_ref[(base_pair + 1) * stride + start + u], ahead.at[u], ahead_sem)
 
     def ready(ref, sem, i):
         pltpu.make_async_copy(ref.at[i], ref.at[i], sem.at[i]).wait()
@@ -107,7 +107,7 @@
         for n, k in enumerate(order):
             proj[g, block(k)] = rows[n * share:(n + 1) * share]
 
-    for m in range(own_pairs):
+    for m in range(pairs_here):
         ready(whole, whole_sem, m)
         total = whole if last else outs[0]
         if first:
@@ -136,14 +136,14 @@
                 term = lax.dot_general(
                     right[r, g].reshape(width, width), proj[g].reshape(width, width),
                     (((0,), (0,)), ((), ())), preferred_element_type=jnp.float32)
-                term = weight_ref[m * stride + start + n * group + g] * term
+                term = weight_ref[(base_pair + m) * stride + start + n * group + g] * term
                 added = term if added is None else added + term
             total[m] = total[m] + added
             return 0
 
         lax.fori_loop(0, rounds, body, 0)
         if last:
-            count = info_ref[m]
+            count = info_ref[base_pair + m]
             row = lax.broadcasted_iota(jnp.int32, (width, width), 0)
             col = lax.broadcasted_iota(jnp.int32, (width, width), 1)
             keep = (row < count) & (col < count)
@@ -156,27 +156,28 @@
 
 
 def run_chunk(
-    start, size, after, first, last, ready_left, near, far, own_pieces, got, slots, weights, info, acc, exch, fock
+    start, size, base_pair, pairs_here, after, first, last, ready_left, near, far, own_pieces, got, slots, weights, info, acc, exch, fock
 ):
     own_pairs = got[0][0].shape[0]
+    taken = ready_left is not None
     ways = len(got) + 1
     width = near.shape[2]
     share = own_pieces.shape[2]
-    units = own_pairs * size
+    units = pairs_here * size
     anywhere = pl.BlockSpec(memory_space=pl.ANY)
     operands = [slots, weights, info, near, far, own_pieces] + [piece for piece, _ in got]
     operands += [exch, fock] if first else [acc]
-    if last:
+    if taken:
         operands.append(ready_left)
     inside = pl.BlockSpec(memory_space=pltpu.VMEM)
     if last:
-        out_shape = [jax.ShapeDtypeStruct((own_pairs, share, width), jnp.bfloat16)] * ways
+        out_shape = [jax.ShapeDtypeStruct((pairs_here, share, width), jnp.bfloat16)] * ways
         out_specs = [inside] * ways
     else:
         out_shape = [jax.ShapeDtypeStruct((own_pairs, width, width), jnp.float32)]
         out_specs = [inside]
     if after:
-        out_shape.append(jax.ShapeDtypeStruct((own_pairs * after, 2, width // 2, width), jnp.bfloat16))
+        out_shape.append(jax.ShapeDtypeStruct((after, 2, width // 2, width), jnp.bfloat16))
         out_specs.append(inside)
     group = max(g for g in (1, 2, 3, 4, 5) if size % g == 0)
     rounds = units // group
@@ -202,12 +203,12 @@
             pair_sems, pair_sems, pair_sems,
         ]
     else:
-        scratch += [pltpu.VMEM((own_pairs, width, width), jnp.float32), pair_sems]
+        scratch += [pltpu.VMEM((pairs_here, width, width), jnp.float32), pair_sems]
     stride = slots.shape[0] // own_pairs
     return pl.pallas_call(
         functools.partial(
-            coupled_kernel, first, last, size, after, start, stride,
-            tuple(o for _, o in got), own_pairs),
+            coupled_kernel, taken, first, last, size, after, start, stride,
+            tuple(o for _, o in got), own_pairs, base_pair, pairs_here),
         out_shape=out_shape,
         in_specs=[anywhere] * len(operands),
         out_specs=out_specs,
@@ -244,9 +245,10 @@
     return whole, lambda block: (place_of(block) - place_of(me) + count) % count
 
 
-def chunk_bounds(length):
-    cuts = [0] + [length * c // 32 for c in CHUNKS] + [length]
-    return list(zip(cuts, cuts[1:]))
+def chunk_bounds(length, own_pairs):
+    cuts = [0] + [length * c // 32 for c in CHUNKS]
+    together = [(0, own_pairs, *cut) for cut in zip(cuts, cuts[1:])]
+    return together + [(m, m + 1, cuts[-1], length) for m in range(own_pairs)]
 
 
 def shards(
@@ -271,22 +273,22 @@
     parts = [masked(amplitudes, 0)]
     parts += [masked(swap(amplitudes, k), k) for k in range(2, ways, 2)]
     half = jnp.concatenate(parts, axis=1)
-    bounds = chunk_bounds(slots_per_pair)
-
-    def moved(k, start, stop):
+    bounds = chunk_bounds(slots_per_pair, own_pairs)
+
+    def moved(k, low, high, start, stop):
         begin = (column ^ k) * own_pairs
         piece = lax.dynamic_slice(
-            intersections, (begin, start, 0, 0), (own_pairs, stop - start, share, width))
+            intersections, (begin + low, start, 0, 0), (high - low, stop - start, share, width))
         if start == 0:
             extra = lax.dynamic_slice_in_dim(exchange_blocks, begin, own_pairs, 0)
             piece = jnp.concatenate([piece, extra[:, None]], axis=1)
         return swap(piece, k)
 
-    beside = moved(1, 0, slots_per_pair)
+    beside = moved(1, 0, own_pairs, 0, slots_per_pair)
     got = []
-    for start, stop in bounds:
-        got.append([(beside, start)] + [
-            (moved(k, start, stop), 0) for k in range(2, ways)])
+    for low, high, start, stop in bounds:
+        got.append([(beside, (low, start))] + [
+            (moved(k, low, high, start, stop), (0, 0)) for k in range(2, ways)])
 
     near, place = gather_pairs(half, count)
     far = swap(near, 1)
@@ -301,15 +303,21 @@
     info = jnp.concatenate([own_counts, own_slots])
 
     acc = ready_left = None
-    for n, (start, stop) in enumerate(bounds):
-        first, last = n == 0, n == len(bounds) - 1
-        after = bounds[n + 1][1] - stop if n == len(bounds) - 2 else 0
+    arrived = [[] for _ in range(ways)]
+    for n, (low, high, start, stop) in enumerate(bounds):
+        last = n >= len(CHUNKS)
+        after = stop - start if last and high < own_pairs else 0
         outs = run_chunk(
-            start, stop - start, after, first, last, ready_left, near, far, intersections,
-            got[n], slots.reshape(-1), weights.reshape(-1), info, acc, exchange_blocks, fock_blocks)
-        acc = outs if last else outs[0]
-        ready_left = outs[1] if after else None
-    arrived = [acc[0]] + [swap(acc[k], k) for k in range(1, ways)]
+            start, stop - start, low, high - low, after, n == 0, last, ready_left, near, far,
+            intersections, got[n], slots.reshape(-1), weights.reshape(-1), info, acc,
+            exchange_blocks, fock_blocks)
+        ready_left = outs[-1] if after else None
+        if last:
+            for k in range(ways):
+                arrived[k].append(outs[k] if k == 0 else swap(outs[k], k))
+        else:
+            acc = outs[0]
+    arrived = [jnp.concatenate(parts) for parts in arrived]
     spots = blocks[:, None, None, None]
     shared = arrived[0][None]
     for k in range(1, ways):

time: 176 us -> 185 us (1.051)
  local copies, waits for them, and re-layouts: 17 us -> 22.4 us
  starting transfers between devices: 19.2 us -> 22.7 us
  waiting for transfers between devices: 109 us -> 106 us
  Pallas kernels: 19.2 us -> 21.3 us
    ppermute x12 -> x17, starting transfers between devices: 11 us -> 14.5 us  [swap(): return lax.ppermute(array, 'cols', [(c, c ^ k) for c in range(ways)])]
    broadcast_in_dim x6, local copies, waits for them, and re-layouts: 0.49 us -> 3.53 us  [shards(): shared = jnp.where(spots == k, arrived[k][None], shared)]
    ppermute x12 -> x17, waiting for transfers between devices: 74.3 us -> 71.4 us  [swap(): return lax.ppermute(array, 'cols', [(c, c ^ k) for c in range(ways)])]
    pallas_call x3 -> x4, Pallas kernels: 19.2 us -> 21.3 us  [run_chunk(): pl.pallas_call(functools.partial(coupled_kernel, taken, first, last, size...]
    unnamed x23 -> x31, local copies, waits for them, and re-layouts: 7.23 us -> 8.27 us
  transfers between devices with their start and end apart: 20 -> 25, of which waited for: 12 -> 9; matrix products, arithmetic and copies ran while one was open for 11% -> 14% of each run, Pallas kernels for 9% -> 10%
where the time goes in v4:
time: 185 us; the launch traced here: 184 us
  waiting for transfers between devices  106 us (57%)
  starting transfers between devices  22.7 us (12%)
  local copies, waits for them, and re-layouts  22.4 us (12%)
  Pallas kernels  21.3 us (12%)
  other arithmetic  11.6 us (6%)
    ppermute x17, waiting for transfers between devices, swap(): return lax.ppermute(array, 'cols', [(c, c ^ k) for c in range(ways)])  71.4 us
    ppermute x3, waiting for transfers between devices, gather_pairs(): forward = lax.ppermute(forward, 'pairs', ahead)  31.2 us
    pallas_call x4, Pallas kernels, run_chunk(): pl.pallas_call(functools.partial(coupled_kernel, taken, first, last, size...  21.3 us
    ppermute x17, starting transfers between devices, swap(): return lax.ppermute(array, 'cols', [(c, c ^ k) for c in range(ways)])  14.5 us
    unnamed x31, local copies, waits for them, and re-layouts  8.27 us
    dynamic_slice x4, local copies, waits for them, and re-layouts, moved(): lax.dynamic_slice(intersections, (begin + low, start, 0, 0), (high - low,...  7.8 us
    ppermute x3, starting transfers between devices, gather_pairs(): forward = lax.ppermute(forward, 'pairs', ahead)  4.78 us
  transfers between devices with their start and end apart: 25, of which 9 were waited for; matrix products, arithmetic and copies ran while one was open for 14% of the time, Pallas kernels for 10%

profile of v4, /device:TPU:0, one launch (start us, length us, event | category | flops | bytes accessed | tf_op | source)
XLA Modules:
  0.0 184.3 jit_solution(4261436584290040622)
XLA Ops:
  0.0 3.0 %collective-permute-start = (bf16[8,64,256]{2,1,0:T(8,128)(2,1)}, bf16[8,64,256]{2,1,0:T(8,128)(2,1)S(1)}, u32[]{:S(2)}, u32[]{:S(2)}) collective-permute-start(bf16[8,64,256]{2,1,0:T(8,128)(2,1)} %param.7), channel_id=1, source_target_pairs={{0,2},{1,3},{2,0},{3,1},{4,6},{5,7},{6,4},{7,5},{8,10},{9,11},{10,... | collective-permute-start | bytes 786440 | tf_op jit(solution)/shard_map/ppermute | solution.py:264
  4.4 5.1 %collective-permute-done = bf16[8,64,256]{2,1,0:T(8,128)(2,1)S(1)} collective-permute-done((bf16[8,64,256]{2,1,0:T(8,128)(2,1)}, bf16[8,64,256]{2,1,0:T(8,128)(2,1)S(1)}, u32[]{:S(2)}, u32[]{:S(2)}) %collective-permute-start) | collective-permute-done | bytes 262176 | tf_op jit(solution)/shard_map/ppermute | solution.py:264
  11.6 1.8 collective-permute-start.4
  13.6 11.1 %collective-permute-done.4 = bf16[8,128,256]{2,1,0:T(8,128)(2,1)S(1)} collective-permute-done((bf16[8,128,256]{2,1,0:T(8,128)(2,1)S(1)}, bf16[8,128,256]{2,1,0:T(8,128)(2,1)S(1)}, u32[]{:S(2)}, u32[]{:S(2)}) %collective-permute-start.4) | collective-permute-done | bytes 524320 | tf_op jit(solution)/shard_map/ppermute | solution.py:234
  24.7 1.5 collective-permute-start.5
  26.7 10.2 %collective-permute-done.5 = bf16[8,128,256]{2,1,0:T(8,128)(2,1)S(1)} collective-permute-done((bf16[8,128,256]{2,1,0:T(8,128)(2,1)S(1)}, bf16[8,128,256]{2,1,0:T(8,128)(2,1)S(1)}, u32[]{:S(2)}, u32[]{:S(2)}) %collective-permute-start.5) | collective-permute-done | bytes 524320 | tf_op jit(solution)/shard_map/ppermute | solution.py:234
  36.9 1.4 collective-permute-start.6
  39.0 10.0 %collective-permute-done.6 = bf16[8,128,256]{2,1,0:T(8,128)(2,1)S(1)} collective-permute-done((bf16[8,128,256]{2,1,0:T(8,128)(2,1)S(1)}, bf16[8,128,256]{2,1,0:T(8,128)(2,1)S(1)}, u32[]{:S(2)}, u32[]{:S(2)}) %collective-permute-start.6) | collective-permute-done | bytes 524320 | tf_op jit(solution)/shard_map/ppermute | solution.py:234
  49.0 1.5 collective-permute-start.7
  53.7 1.7 collective-permute-done.7
  56.1 1.6 collective-permute-done.8
  61.1 1.7 constant_dynamic-slice_fusion.8
  62.8 1.5 pad_maximum_fusion
  64.8 1.9 %constant_dynamic-slice_fusion.2 = (bf16[2,20,64,256]{3,2,1,0:T(8,128)(2,1)S(1)}, bf16[2,20,64,256]{3,2,1,0:T(8,128)(2,1)S(1)}) fusion(bf16[8,32,64,256]{3,2,1,0:T(8,128)(2,1)} %own.7, s32[]{:T(128)S(6)} %select_n.115, s32[]{:T(128)S(6)} %select_n.114), kind=kLoop, calls=%fused_computation.28 | loop fusion | bytes 5242888 | tf_op jit(solution)/shard_map/dynamic_slice | solution.py:280
  66.9 1.6 collective-permute-start.15
  69.6 2.3 %constant_dynamic-slice_fusion.4 = (bf16[2,8,64,256]{3,2,1,0:T(8,128)(2,1)}, bf16[2,8,64,256]{3,2,1,0:T(8,128)(2,1)}) fusion(bf16[8,32,64,256]{3,2,1,0:T(8,128)(2,1)} %own.7, s32[]{:T(128)S(6)} %select_n.115, s32[]{:T(128)S(6)} %select_n.114), kind=kLoop, calls=%fused_computation.30 | loop fusion | bytes 2097160 | tf_op jit(solution)/shard_map/dynamic_slice | solution.py:280
  71.9 1.4 collective-permute-start.13
  75.1 64.7 %collective-permute-done.13.refs_1_ = bf16[2,8,64,256]{3,2,1,0:T(8,128)(2,1)} collective-permute-done((bf16[2,8,64,256]{3,2,1,0:T(8,128)(2,1)}, bf16[2,8,64,256]{3,2,1,0:T(8,128)(2,1)}, u32[]{:S(2)}, u32[]{:S(2)}) %collective-permute-start.13) | collective-permute-done | bytes 524320 | tf_op jit(solution)/shard_map/ppermute | solution.py:264
  147.3 1.9 %constant_dynamic-slice_fusion.6 = (bf16[1,4,64,256]{3,2,1,0:T(8,128)(2,1)}, bf16[1,4,64,256]{3,2,1,0:T(8,128)(2,1)}, bf16[1,4,64,256]{3,2,1,0:T(8,128)(2,1)}, bf16[1,4,64,256]{3,2,1,0:T(8,128)(2,1)}) fusion(bf16[8,32,64,256]{3,2,1,0:T(8,128)(2,1)} %own.7, s32[]{:T(128)S(6)} %select_n.115, s32[]{:T(128)S(6)} %select_n.116, s32[]{:T(128)S(6)} %select_n.114, ...), kind=kLoop, calls=%fused_computation.32 | loop fusion | bytes 1048592 | tf_op jit(solution)/shard_map/dynamic_slice | solution.py:280
  150.4 1.5 collective-permute-start.12
  153.3 9.4 %coupled.4.refs_3_ = f32[2,256,256]{2,1,0:T(8,128)} custom-call(s32[64]{0:T(128)} %reshape.115.slots, f32[64]{0:T(128)} %reshape.116.weights, s32[4]{0:T(128)} %pad_add_fusion.info, bf16[64,128,256]{2,1,0:T(8,128)(2,1)} %constant_dynamic-update-slice_fusion.near, bf16[64,128,256]{2,1,0:T(8,128)(2,1)} %collective-permute-done.9.far, ...), custom_call_target="tpu_custom_call" | custom-call | flops 2684354560 | bytes 10485760 | tf_op jit(solution)/shard_map/coupled/pallas_call | solution.py:208
  162.7 5.4 %coupled.5.refs_3_ = f32[2,256,256]{2,1,0:T(8,128)} custom-call(s32[64]{0:T(128)} %reshape.115.slots, f32[64]{0:T(128)} %reshape.116.weights, s32[4]{0:T(128)} %pad_add_fusion.info, bf16[64,128,256]{2,1,0:T(8,128)(2,1)} %constant_dynamic-update-slice_fusion.near, bf16[64,128,256]{2,1,0:T(8,128)(2,1)} %collective-permute-done.9.far, ...), custom_call_target="tpu_custom_call" | custom-call | flops 1073741824 | bytes 4194304 | tf_op jit(solution)/shard_map/coupled/pallas_call | solution.py:208
  169.5 3.6 %coupled.6 = (bf16[1,64,256]{2,1,0:T(8,128)(2,1)}, bf16[1,64,256]{2,1,0:T(8,128)(2,1)}, bf16[1,64,256]{2,1,0:T(8,128)(2,1)}, bf16[1,64,256]{2,1,0:T(8,128)(2,1)}, bf16[4,2,128,256]{3,2,1,0:T(8,128)(2,1)}) custom-call(s32[64]{0:T(128)} %reshape.115.slots, f32[64]{0:T(128)} %reshape.116.weights, s32[4]{0:T(128)} %pad_add_fusion.info, ...), custom_call_target="tpu_custom_call" | custom-call | flops 268435456 | bytes 1048576 | tf_op jit(solution)/shard_map/coupled/pallas_call | solution.py:208
  173.8 2.7 %coupled.7 = (bf16[1,64,256]{2,1,0:T(8,128)(2,1)}, bf16[1,64,256]{2,1,0:T(8,128)(2,1)}, bf16[1,64,256]{2,1,0:T(8,128)(2,1)}, bf16[1,64,256]{2,1,0:T(8,128)(2,1)}) custom-call(s32[64]{0:T(128)} %reshape.115.slots, f32[64]{0:T(128)} %reshape.116.weights, s32[4]{0:T(128)} %pad_add_fusion.info, bf16[64,128,256]{2,1,0:T(8,128)(2,1)} %constant_dynamic-update-slice_fusion.near, ...), custom_call_target="tpu_custom_call" | custom-call | flops 268435456 | bytes 1048576 | tf_op jit(solution)/shard_map/coupled/pallas_call | solution.py:208
  (97 shorter events, 35.5 us)
Async XLA Ops:
  0.0 9.5 %collective-permute-start = (bf16[8,64,256]{2,1,0:T(8,128)(2,1)}, bf16[8,64,256]{2,1,0:T(8,128)(2,1)S(1)}, u32[]{:S(2)}, u32[]{:S(2)}) collective-permute-start(bf16[8,64,256]{2,1,0:T(8,128)(2,1)} %param.7), channel_id=1, source_target_pairs={{0,2},{1,3},{2,0},{3,1},{4,6},{5,7},{6,4},{7,5},{8,10},{9,11},{10,... | collective-permute-start | bytes 786440 | tf_op jit(solution)/shard_map/ppermute | solution.py:264
  11.6 13.1 %collective-permute-start.4 = (bf16[8,128,256]{2,1,0:T(8,128)(2,1)S(1)}, bf16[8,128,256]{2,1,0:T(8,128)(2,1)S(1)}, u32[]{:S(2)}, u32[]{:S(2)}) collective-permute-start(bf16[8,128,256]{2,1,0:T(8,128)(2,1)S(1)} %get-tuple-element.31), channel_id=1, source_target_pairs={{0,8},{8,16},{16,24},{24,28},{28,20},{20,12},{12,4},{4,0},{1,9},{9... | collective-permute-start | bytes 1572872 | tf_op jit(solution)/shard_map/ppermute | solution.py:234
  13.4 12.8 %collective-permute-start.1 = (bf16[8,128,256]{2,1,0:T(8,128)(2,1)S(1)}, bf16[8,128,256]{2,1,0:T(8,128)(2,1)S(1)}, u32[]{:S(2)}, u32[]{:S(2)}) collective-permute-start(bf16[8,128,256]{2,1,0:T(8,128)(2,1)S(1)} %get-tuple-element.31), channel_id=1, source_target_pairs={{8,0},{16,8},{24,16},{28,24},{20,28},{12,20},{4,12},{0,4},{9,1},{1... | collective-permute-start | bytes 1572872 | tf_op jit(solution)/shard_map/ppermute | solution.py:235
  24.7 12.2 %collective-permute-start.5 = (bf16[8,128,256]{2,1,0:T(8,128)(2,1)S(1)}, bf16[8,128,256]{2,1,0:T(8,128)(2,1)S(1)}, u32[]{:S(2)}, u32[]{:S(2)}) collective-permute-start(bf16[8,128,256]{2,1,0:T(8,128)(2,1)S(1)} %collective-permute-done.4), channel_id=1, source_target_pairs={{0,8},{8,16},{16,24},{24,28},{28,20},{20,12},{12,4},{4,0},{1,9},{9... | collective-permute-start | bytes 1572872 | tf_op jit(solution)/shard_map/ppermute | solution.py:234
  26.2 12.1 %collective-permute-start.2 = (bf16[8,128,256]{2,1,0:T(8,128)(2,1)S(1)}, bf16[8,128,256]{2,1,0:T(8,128)(2,1)S(1)}, u32[]{:S(2)}, u32[]{:S(2)}) collective-permute-start(bf16[8,128,256]{2,1,0:T(8,128)(2,1)S(1)} %collective-permute-done.1), channel_id=1, source_target_pairs={{8,0},{16,8},{24,16},{28,24},{20,28},{12,20},{4,12},{0,4},{9,1},{1... | collective-permute-start | bytes 1572872 | tf_op jit(solution)/shard_map/ppermute | solution.py:235
  36.9 12.0 %collective-permute-start.6 = (bf16[8,128,256]{2,1,0:T(8,128)(2,1)S(1)}, bf16[8,128,256]{2,1,0:T(8,128)(2,1)S(1)}, u32[]{:S(2)}, u32[]{:S(2)}) collective-permute-start(bf16[8,128,256]{2,1,0:T(8,128)(2,1)S(1)} %collective-permute-done.5), channel_id=1, source_target_pairs={{0,8},{8,16},{16,24},{24,28},{28,20},{20,12},{12,4},{4,0},{1,9},{9... | collective-permute-start | bytes 1572872 | tf_op jit(solution)/shard_map/ppermute | solution.py:234
  38.3 13.0 %collective-permute-start.3 = (bf16[8,128,256]{2,1,0:T(8,128)(2,1)S(1)}, bf16[8,128,256]{2,1,0:T(8,128)(2,1)S(1)}, u32[]{:S(2)}, u32[]{:S(2)}) collective-permute-start(bf16[8,128,256]{2,1,0:T(8,128)(2,1)S(1)} %collective-permute-done.2), channel_id=1, source_target_pairs={{8,0},{16,8},{24,16},{28,24},{20,28},{12,20},{4,12},{0,4},{9,1},{1... | collective-permute-start | bytes 1572872 | tf_op jit(solution)/shard_map/ppermute | solution.py:235
  49.0 6.4 %collective-permute-start.7 = (bf16[4,128,256]{2,1,0:T(8,128)(2,1)S(1)}, bf16[4,128,256]{2,1,0:T(8,128)(2,1)S(1)}, u32[]{:S(2)}, u32[]{:S(2)}) collective-permute-start(bf16[4,128,256]{2,1,0:T(8,128)(2,1)S(1)} %slice.8), channel_id=1, source_target_pairs={{0,8},{8,16},{16,24},{24,28},{28,20},{20,12},{12,4},{4,0},{1,9},{9... | collective-permute-start | bytes 786440 | tf_op jit(solution)/shard_map/ppermute | solution.py:238
  51.3 6.4 %collective-permute-start.8 = (bf16[4,128,256]{2,1,0:T(8,128)(2,1)S(1)}, bf16[4,128,256]{2,1,0:T(8,128)(2,1)S(1)}, u32[]{:S(2)}, u32[]{:S(2)}) collective-permute-start(bf16[4,128,256]{2,1,0:T(8,128)(2,1)S(1)} %slice.9), channel_id=1, source_target_pairs={{8,0},{16,8},{24,16},{28,24},{20,28},{12,20},{4,12},{0,4},{9,1},{1... | collective-permute-start | bytes 786440 | tf_op jit(solution)/shard_map/ppermute | solution.py:239
  61.0 91.4 %collective-permute-start.9 = (bf16[64,128,256]{2,1,0:T(8,128)(2,1)}, bf16[64,128,256]{2,1,0:T(8,128)(2,1)}, u32[]{:S(2)}, u32[]{:S(2)}) collective-permute-start(bf16[64,128,256]{2,1,0:T(8,128)(2,1)} %constant_dynamic-update-slice_fusion.near), channel_id=1, source_target_pairs={{0,1},{1,0},{2,3},{3,2},{4,5},{5,4},{6,7},{7,6},{8,9},{9,8},{10,11... | collective-permute-start | bytes 12582920 | tf_op jit(solution)/shard_map/ppermute | solution.py:264
  64.3 87.6 %collective-permute-start.10 = (bf16[2,33,64,256]{3,2,1,0:T(8,128)(2,1)}, bf16[2,33,64,256]{3,2,1,0:T(8,128)(2,1)S(1)}, u32[]{:S(2)}, u32[]{:S(2)}) collective-permute-start(bf16[2,33,64,256]{3,2,1,0:T(8,128)(2,1)} %pad_maximum_fusion), channel_id=1, source_target_pairs={{0,1},{1,0},{2,3},{3,2},{4,5},{5,4},{6,7},{7,6},{8,9},{9,8},{10,11... | collective-permute-start | bytes 6488072 | tf_op jit(solution)/shard_map/ppermute | solution.py:264
  66.9 82.3 %collective-permute-start.15 = (bf16[2,21,64,256]{3,2,1,0:T(8,128)(2,1)S(1)}, bf16[2,21,64,256]{3,2,1,0:T(8,128)(2,1)}, u32[]{:S(2)}, u32[]{:S(2)}) collective-permute-start(bf16[2,21,64,256]{3,2,1,0:T(8,128)(2,1)S(1)} %pad_maximum_fusion.1), channel_id=1, source_target_pairs={{0,2},{1,3},{2,0},{3,1},{4,6},{5,7},{6,4},{7,5},{8,10},{9,11},{10,... | collective-permute-start | bytes 4128776 | tf_op jit(solution)/shard_map/ppermute | solution.py:264
  69.6 80.8 %collective-permute-start.16 = (bf16[2,21,64,256]{3,2,1,0:T(8,128)(2,1)}, bf16[2,21,64,256]{3,2,1,0:T(8,128)(2,1)}, u32[]{:S(2)}, u32[]{:S(2)}) collective-permute-start(bf16[2,21,64,256]{3,2,1,0:T(8,128)(2,1)} %pad_maximum_fusion.2), channel_id=1, source_target_pairs={{0,3},{1,2},{2,1},{3,0},{4,7},{5,6},{6,5},{7,4},{8,11},{9,10},{10,... | collective-permute-start | bytes 4128776 | tf_op jit(solution)/shard_map/ppermute | solution.py:264
  71.9 67.9 %collective-permute-start.13 = (bf16[2,8,64,256]{3,2,1,0:T(8,128)(2,1)}, bf16[2,8,64,256]{3,2,1,0:T(8,128)(2,1)}, u32[]{:S(2)}, u32[]{:S(2)}) collective-permute-start(bf16[2,8,64,256]{3,2,1,0:T(8,128)(2,1)} %get-tuple-element.30), channel_id=1, source_target_pairs={{0,2},{1,3},{2,0},{3,1},{4,6},{5,7},{6,4},{7,5},{8,10},{9,11},{10,... | collective-permute-start | bytes 1572872 | tf_op jit(solution)/shard_map/ppermute | solution.py:264
  139.9 22.9 %collective-permute-start.14 = (bf16[2,8,64,256]{3,2,1,0:T(8,128)(2,1)}, bf16[2,8,64,256]{3,2,1,0:T(8,128)(2,1)}, u32[]{:S(2)}, u32[]{:S(2)}) collective-permute-start(bf16[2,8,64,256]{3,2,1,0:T(8,128)(2,1)} %get-tuple-element.29), channel_id=1, source_target_pairs={{0,3},{1,2},{2,1},{3,0},{4,7},{5,6},{6,5},{7,4},{8,11},{9,10},{10,... | collective-permute-start | bytes 1572872 | tf_op jit(solution)/shard_map/ppermute | solution.py:264
  149.2 19.0 %collective-permute-start.11 = (bf16[1,4,64,256]{3,2,1,0:T(8,128)(2,1)}, bf16[1,4,64,256]{3,2,1,0:T(8,128)(2,1)S(1)}, u32[]{:S(2)}, u32[]{:S(2)}) collective-permute-start(bf16[1,4,64,256]{3,2,1,0:T(8,128)(2,1)} %get-tuple-element.25), channel_id=1, source_target_pairs={{0,2},{1,3},{2,0},{3,1},{4,6},{5,7},{6,4},{7,5},{8,10},{9,11},{10,... | collective-permute-start | bytes 393224 | tf_op jit(solution)/shard_map/ppermute | solution.py:264
  150.4 17.8 %collective-permute-start.12 = (bf16[1,4,64,256]{3,2,1,0:T(8,128)(2,1)}, bf16[1,4,64,256]{3,2,1,0:T(8,128)(2,1)S(1)}, u32[]{:S(2)}, u32[]{:S(2)}) collective-permute-start(bf16[1,4,64,256]{3,2,1,0:T(8,128)(2,1)} %get-tuple-element.23), channel_id=1, source_target_pairs={{0,3},{1,2},{2,1},{3,0},{4,7},{5,6},{6,5},{7,4},{8,11},{9,10},{10,... | collective-permute-start | bytes 393224 | tf_op jit(solution)/shard_map/ppermute | solution.py:264
  151.9 21.2 %collective-permute-start.18 = (bf16[1,4,64,256]{3,2,1,0:T(8,128)(2,1)}, bf16[1,4,64,256]{3,2,1,0:T(8,128)(2,1)S(1)}, u32[]{:S(2)}, u32[]{:S(2)}) collective-permute-start(bf16[1,4,64,256]{3,2,1,0:T(8,128)(2,1)} %get-tuple-element.24), channel_id=1, source_target_pairs={{0,2},{1,3},{2,0},{3,1},{4,6},{5,7},{6,4},{7,5},{8,10},{9,11},{10,... | collective-permute-start | bytes 393224 | tf_op jit(solution)/shard_map/ppermute | solution.py:264
  152.5 20.7 %collective-permute-start.19 = (bf16[1,4,64,256]{3,2,1,0:T(8,128)(2,1)}, bf16[1,4,64,256]{3,2,1,0:T(8,128)(2,1)S(1)}, u32[]{:S(2)}, u32[]{:S(2)}) collective-permute-start(bf16[1,4,64,256]{3,2,1,0:T(8,128)(2,1)} %get-tuple-element.26), channel_id=1, source_target_pairs={{0,3},{1,2},{2,1},{3,0},{4,7},{5,6},{6,5},{7,4},{8,11},{9,10},{10,... | collective-permute-start | bytes 393224 | tf_op jit(solution)/shard_map/ppermute | solution.py:264
  176.6 4.8 %collective-permute-start.20 = (bf16[1,64,256]{2,1,0:T(8,128)(2,1)}, bf16[1,64,256]{2,1,0:T(8,128)(2,1)S(1)}, u32[]{:S(2)}, u32[]{:S(2)}) collective-permute-start(bf16[1,64,256]{2,1,0:T(8,128)(2,1)} %get-tuple-element.16), channel_id=1, source_target_pairs={{0,3},{1,2},{2,1},{3,0},{4,7},{5,6},{6,5},{7,4},{8,11},{9,10},{10,... | collective-permute-start | bytes 98312 | tf_op jit(solution)/shard_map/ppermute | solution.py:264
  177.7 4.1 %collective-permute-start.17 = (bf16[1,64,256]{2,1,0:T(8,128)(2,1)S(1)}, bf16[1,64,256]{2,1,0:T(8,128)(2,1)S(1)}, u32[]{:S(2)}, u32[]{:S(2)}) collective-permute-start(bf16[1,64,256]{2,1,0:T(8,128)(2,1)S(1)} %copy-done.11), channel_id=1, source_target_pairs={{0,3},{1,2},{2,1},{3,0},{4,7},{5,6},{6,5},{7,4},{8,11},{9,10},{10,... | collective-permute-start | bytes 98312 | tf_op jit(solution)/shard_map/ppermute | solution.py:264
  178.4 4.5 %collective-permute-start.22 = (bf16[1,64,256]{2,1,0:T(8,128)(2,1)}, bf16[1,64,256]{2,1,0:T(8,128)(2,1)S(1)}, u32[]{:S(2)}, u32[]{:S(2)}) collective-permute-start(bf16[1,64,256]{2,1,0:T(8,128)(2,1)} %get-tuple-element.18), channel_id=1, source_target_pairs={{0,2},{1,3},{2,0},{3,1},{4,6},{5,7},{6,4},{7,5},{8,10},{9,11},{10,... | collective-permute-start | bytes 98312 | tf_op jit(solution)/shard_map/ppermute | solution.py:264
  179.2 4.1 %collective-permute-start.21 = (bf16[1,64,256]{2,1,0:T(8,128)(2,1)S(1)}, bf16[1,64,256]{2,1,0:T(8,128)(2,1)S(1)}, u32[]{:S(2)}, u32[]{:S(2)}) collective-permute-start(bf16[1,64,256]{2,1,0:T(8,128)(2,1)S(1)} %copy-done.10), channel_id=1, source_target_pairs={{0,2},{1,3},{2,0},{3,1},{4,6},{5,7},{6,4},{7,5},{8,10},{9,11},{10,... | collective-permute-start | bytes 98312 | tf_op jit(solution)/shard_map/ppermute | solution.py:264
  180.5 2.9 %collective-permute-start.24 = (bf16[1,64,256]{2,1,0:T(8,128)(2,1)}, bf16[1,64,256]{2,1,0:T(8,128)(2,1)S(1)}, u32[]{:S(2)}, u32[]{:S(2)}) collective-permute-start(bf16[1,64,256]{2,1,0:T(8,128)(2,1)} %get-tuple-element.20), channel_id=1, source_target_pairs={{0,1},{1,0},{2,3},{3,2},{4,5},{5,4},{6,7},{7,6},{8,9},{9,8},{10,11... | collective-permute-start | bytes 98312 | tf_op jit(solution)/shard_map/ppermute | solution.py:264
  (13 other events, 227.3 us)
